TPU v7x, 256 devices: a whole 4x4x8 slice. The times are simulated.
256 devices in a mesh: slab: 128 (over z, y_lo, x, core), layer: 2 (over y_hi).
Axes of the slice: x: 4, y: 4 (y_hi: 2, y_lo: 2; y = y_hi * 2 + y_lo), z: 8, core: 2. Of those that a mesh axis runs over, the one named last changes fastest.
Arguments:
- nodal_field: float32 [2, 8192, 4, 4, 512], P('layer', 'slab'), may hold values from -6 to 6
- metric: float32 [2, 8192, 4, 4, 3, 512], P('layer', 'slab'), may hold values from 0.25 to 2
- slab_ids: int32 [8192], replicated, may hold values from 0 to 8191, as said below
- face_map: int32 [8192, 1024], P('slab'), may hold values from 0 to 1023, as said below
Outputs:
- assembled: float32 [2, 8192, 4, 4, 512], P('layer', 'slab')
Inputs may be any that keep to these rules, and one draw needn't show every extreme that they name: slab_ids is a permutation of 0 to 8191; positions p of one device are those with p // 64 equal to its index along slab, and for one rotation R every device holds exactly the slabs g with (g + R) mod 128 equal to its index, in any order of its positions, so slab (g + 1) mod 8192 always sits on the next device along slab, cyclically. Each row of face_map is a permutation of 0 to 1023: either the identity, or the map that reverses y, sending (ez, ey, c, b) to (ez, 3 - ey, c, 7 - b); z order is never changed.
All inputs are finite; a program needn't handle non-finite values.
Results may differ from a plain program's by a relative error of at most 0.00005.
Values sent between devices are 32-bit elements; how exact they have to be, the bound alone decides.
A program may use at most 192 MiB of HBM per device.

v0:
```python
import functools

import jax
import jax.numpy as jnp
import numpy as np
from jax import lax
from jax.experimental import pallas as pl
from jax.experimental.pallas import tpu as pltpu
from jax.sharding import PartitionSpec as P

P_SIZE = 8
PTS = 512
EY = 4
EZ = 4
CHUNK = 8
F32 = jnp.float32
BF16 = jnp.bfloat16
MESH = pl.DeviceIdType.MESH


def legendre_pair(gll_nodes, degree):
    lower_poly = gll_nodes * 0.0 + 1.0
    upper_poly = gll_nodes.copy()
    for poly_order in range(2, degree + 1):
        lower_poly, upper_poly = (
            upper_poly,
            ((2 * poly_order - 1) * gll_nodes * upper_poly - (poly_order - 1) * lower_poly)
            / poly_order,
        )
    return (lower_poly, upper_poly)


def gll_tables():
    degree = P_SIZE - 1
    gll_nodes = -np.cos(np.pi * np.arange(P_SIZE) / degree)
    for newton_sweep in range(100):
        lower_poly, upper_poly = legendre_pair(gll_nodes, degree)
        gll_nodes = gll_nodes - (gll_nodes * upper_poly - lower_poly) / ((degree + 1) * upper_poly)
    lower_poly, upper_poly = legendre_pair(gll_nodes, degree)
    quad_weights = 2.0 / (degree * (degree + 1) * upper_poly * upper_poly)
    identity = np.eye(P_SIZE)
    differ = gll_nodes[:, None] - gll_nodes[None, :] + identity
    derivative = upper_poly[:, None] / (upper_poly[None, :] * differ)
    derivative = derivative * (1.0 - identity)
    derivative[0, 0] = -degree * (degree + 1) / 4.0
    derivative[degree, degree] = degree * (degree + 1) / 4.0
    return derivative, quad_weights


def parts(table):
    high = np.asarray(table, np.float32).astype(BF16)
    low = (table - high.astype(np.float64)).astype(np.float32).astype(BF16)
    return high, low


def constant_tables():
    derivative, rho = gll_tables()
    eye = np.eye(P_SIZE)
    pair = np.eye(2)
    x_in = np.kron(pair, np.kron(eye, derivative.T))
    y_in = np.kron(pair, np.kron(derivative.T, eye))
    x_out = np.kron(pair, np.kron(eye, derivative))
    y_out = np.kron(pair, np.kron(derivative, eye))
    high, low = parts(np.concatenate([x_in, y_in], 1))
    matrices = [np.concatenate([part, part], 0) for part in (high, low)]
    for table in (x_out, y_out):
        both = np.concatenate(parts(table), 1)
        matrices.append(np.concatenate([both, both], 0))
    sub = np.arange(8)[:, None] // 4
    lane = np.arange(128)[None, :]
    c_low = 2 * sub + lane // 64
    vectors = []
    for table in (derivative, derivative.T):
        for sign in (1.0, -1.0):
            for move in (0, 2, 1, 3):
                other = c_low ^ move
                vectors.append((table[c_low, other] + sign * table[c_low, 7 - other]) / 2)
    plane = rho[lane // 8 % 8] * rho[lane % 8]
    for half in range(2):
        vectors.append(rho[4 * half + c_low] * plane)
    return np.stack(matrices), np.stack(vectors).astype(np.float32)


def turn(value, shift):
    return pltpu.roll(value, shift % 128, axis=value.ndim - 1) if shift % 128 else value


def slide(value, shift):
    return pltpu.roll(value, shift % 8, axis=value.ndim - 2)


def mirror(value):
    return slide(turn(value, 64), 4)


def iotas():
    sub = lax.broadcasted_iota(jnp.int32, (8, 128), 0)
    lane = lax.broadcasted_iota(jnp.int32, (8, 128), 1)
    return sub, lane


def split(value):
    high = value.astype(BF16)
    low = (value - high.astype(F32)).astype(BF16)
    return jnp.concatenate([high, low], axis=-1)


def along_z(low, high, table_ref, start):
    back = mirror(high)
    halves = []
    for value, first in ((low + back, start), (low - back, start + 4)):
        moved = slide(value, 4)
        total = table_ref[first] * value + table_ref[first + 1] * moved
        total += table_ref[first + 2] * turn(value, 64) + table_ref[first + 3] * turn(moved, 64)
        halves.append(total)
    even, odd = halves
    return even + odd, mirror(odd - even)


def flip_faces(value, sub, lane):
    value = jnp.take_along_axis(value, sub ^ 3, axis=0)
    return jnp.take_along_axis(value, lane ^ 56, axis=1)


def edge_mask(sub, lane, slot):
    base = jnp.where(sub < 4, 0, 71)
    return ((lane - base - slot) & 71) == 0


def chunk_local(u_ref, m_ref, mat_ref, vec_ref, flip_mask, sub, lane):
    count = u_ref.shape[0]
    rows = count * EZ * 2 * 8
    u = u_ref[...].reshape(rows, 128)
    both = split(u)
    grads = jnp.dot(both, mat_ref[0], preferred_element_type=F32)
    grads += jnp.dot(both, mat_ref[1], preferred_element_type=F32)
    weights = [vec_ref[16], vec_ref[17]]
    flux_x, flux_y, out_z = [], [], []
    for s in range(count):
        for ez in range(EZ):
            at = (s * EZ + ez) * 16
            pieces = along_z(u_ref[s, ez, 0], u_ref[s, ez, 1], vec_ref, 0)
            flux_z = [pieces[h] * (weights[h] * m_ref[s, ez, 2, h]) for h in range(2)]
            out_z.append(along_z(flux_z[0], flux_z[1], vec_ref, 8))
            for h in range(2):
                grad = grads[at + 8 * h : at + 8 * h + 8]
                flux_x.append(grad[:, :128] * (weights[h] * m_ref[s, ez, 0, h]))
                flux_y.append(grad[:, 128:] * (weights[h] * m_ref[s, ez, 1, h]))
    result = jnp.dot(split(jnp.concatenate(flux_x, 0)), mat_ref[2], preferred_element_type=F32)
    result += jnp.dot(split(jnp.concatenate(flux_y, 0)), mat_ref[3], preferred_element_type=F32)

    b = (lane >> 3) & 7
    a = lane & 7
    ey = sub & 3
    high_b = (b == 7) & (ey < 3)
    low_b = (b == 0) & (ey > 0)
    bottom = (sub < 4) & (lane < 64)
    top = (sub >= 4) & (lane >= 64)
    diagonal = bottom | top
    local, lefts, rights, z_own = [], [], [], []
    for s in range(count):
        block = []
        for ez in range(EZ):
            for h in range(2):
                at = (s * EZ + ez) * 16 + 8 * h
                v = result[at : at + 8, :128] + result[at : at + 8, 128:] + out_z[s * EZ + ez][h]
                after = turn(slide(v, -1), 56)
                before = turn(slide(v, 1), -56)
                block.append(v + jnp.where(high_b, after, jnp.where(low_b, before, 0.0)))
        for ez in range(EZ - 1):
            upper, lower = block[2 * ez + 1], block[2 * ez + 2]
            total = mirror(upper) + lower
            block[2 * ez + 2] = jnp.where(bottom, total, lower)
            block[2 * ez + 1] = jnp.where(top, mirror(total), upper)
        left, right = block[0], turn(block[7], 0)
        for j in range(1, 8):
            left = jnp.where(a == j, turn(block[j], j), left)
        for j in range(7):
            right = jnp.where(a == j, turn(block[j], j - 7), right)
        right = jnp.where(flip_mask(s), flip_faces(right, sub, lane), right)
        local.append(block)
        lefts.append(left)
        rights.append(right)
        z_own.append(jnp.where(bottom, block[0], block[7]))
    z_pairs = [
        jnp.where(diagonal, z_own[s], turn(z_own[s + 1], 64)) for s in range(0, count, 2)
    ]
    edges = []
    for faces in (lefts, rights):
        packed = faces[0]
        for s in range(1, count):
            packed = jnp.where(edge_mask(sub, lane, s), turn(faces[s], s), packed)
        moved = slide(packed, 4)
        edges.append(jnp.where(sub < 4, turn(moved, -71), turn(moved, 71)))
    return local, lefts, rights, z_pairs, edges


def chunk_final(local_ref, left_in, right_in, z_in, put):
    sub, lane = iotas()
    a = lane & 7
    bottom = (sub < 4) & (lane < 64)
    top = (sub >= 4) & (lane >= 64)
    count = local_ref.shape[0]
    for s in range(count):
        left, right, z = left_in(s), right_in(s), z_in(s)
        for j in range(8):
            v = local_ref[s, j // 2, j % 2]
            v += jnp.where(a == 0, turn(left, -j), jnp.where(a == 7, turn(right, 7 - j), 0.0))
            if j == 0:
                v += jnp.where(bottom, z, 0.0)
            if j == 7:
                v += jnp.where(top, z, 0.0)
            put(s, j, v)


def compute_kernel(u_ref, m_ref, mat_ref, vec_ref, fm_ref, ids_ref, local_ref, left_ref, right_ref, z_ref, el_ref, er_ref, inv_ref):
    step = pl.program_id(0)
    sub, lane = iotas()
    cycle = lax.axis_size("slab")
    device = lax.axis_index("slab")
    here = pl.num_programs(0) * CHUNK
    after = lax.rem(device + 1, cycle) * here
    before = lax.rem(device + cycle - 1, cycle) * here
    shift = cycle.bit_length() - 1
    for t in range(CHUNK):
        place = step * CHUNK + t
        inv_ref[ids_ref[before + place] >> shift] = place
        inv_ref[here + (ids_ref[after + place] >> shift)] = place

    def flip_mask(s):
        return fm_ref[s : s + 1, :] != lane

    local, lefts, rights, z_pairs, edges = chunk_local(
        u_ref, m_ref, mat_ref, vec_ref, flip_mask, sub, lane
    )
    for s in range(CHUNK):
        for j in range(8):
            local_ref[s, j // 2, j % 2] = local[s][j]
        left_ref[s] = lefts[s]
        right_ref[s] = rights[s]
    for s in range(CHUNK // 2):
        z_ref[s] = z_pairs[s]
    el_ref[0] = edges[0]
    er_ref[0] = edges[1]


def exchange_kernel(left, right, z, el, er, left_in, right_in, z_in, el_in, er_in, send_sem, recv_sem):
    cycle = lax.axis_size("slab")
    me = lax.axis_index("slab")
    layer = lax.axis_index("layer")
    after, before = lax.rem(me + 1, cycle), lax.rem(me + cycle - 1, cycle)
    other = 1 - layer
    peers = [(after, layer), (before, layer), (me, other), (after, other), (before, other)]
    barrier = pltpu.get_barrier_semaphore()
    for s, l in peers:
        pl.semaphore_signal(barrier, inc=1, device_id={"slab": s, "layer": l}, device_id_type=MESH)
    pl.semaphore_wait(barrier, 5)
    jobs = [(right, right_in), (left, left_in), (z, z_in), (er, er_in), (el, el_in)]
    copies = []
    for i, ((src, dst), (s, l)) in enumerate(zip(jobs, peers)):
        copies.append(
            pltpu.make_async_remote_copy(
                src_ref=src,
                dst_ref=dst,
                send_sem=send_sem.at[i],
                recv_sem=recv_sem.at[i],
                device_id={"slab": s, "layer": l},
                device_id_type=MESH,
            )
        )
    for copy in copies:
        copy.start()
    for copy in copies:
        copy.wait()


def final_kernel(local_ref, left_in, right_in, z_in, el_in, er_in, fm_ref, ids_ref, inv_ref, out_ref):
    step = pl.program_id(0)
    sub, lane = iotas()
    cycle = lax.axis_size("slab")
    device = lax.axis_index("slab")
    here = pl.num_programs(0) * CHUNK
    total = cycle * here
    shift = cycle.bit_length() - 1
    own = device * here + step * CHUNK
    on_edge = edge_mask(sub, lane, 0)

    def fetch(face_ref, edge_ref, at):
        packed = pltpu.roll(edge_ref[at >> 3], (128 - (at & 7)) & 127, axis=1)
        return face_ref[at] + jnp.where(on_edge, packed, 0.0)

    def get_left(s):
        at = inv_ref[lax.rem(ids_ref[own + s] + total - 1, total) >> shift]
        return fetch(right_in, er_in, at)

    def get_right(s):
        at = inv_ref[here + (lax.rem(ids_ref[own + s] + 1, total) >> shift)]
        value = fetch(left_in, el_in, at)
        return jnp.where(fm_ref[s : s + 1, :] != lane, flip_faces(value, sub, lane), value)

    def get_z(s):
        value = slide(z_in[s // 2], 4)
        return value if s % 2 else turn(value, 64)

    def put(s, j, value):
        out_ref[s, j // 2, j % 2] = value

    chunk_final(local_ref, get_left, get_right, get_z, put)


def body(nodal_field, metric, slab_ids, face_map):
    count = nodal_field.shape[1]
    steps = count // CHUNK
    u = nodal_field.reshape(count, EZ, EY, 2, 2, 128).transpose(0, 1, 3, 4, 2, 5)
    u = u.reshape(count, EZ, 2, 8, 128)
    m = metric.reshape(count, EZ, EY, 3, 2, 2, 128).transpose(0, 1, 3, 4, 5, 2, 6)
    m = m.reshape(count, EZ, 3, 2, 8, 128)
    matrices, vectors = constant_tables()
    matrices, vectors = jnp.asarray(matrices), jnp.asarray(vectors)
    smem = pl.BlockSpec(memory_space=pltpu.SMEM)
    vmem = pl.BlockSpec(memory_space=pltpu.VMEM)
    blocks = pl.BlockSpec((CHUNK, EZ, 2, 8, 128), lambda i: (i, 0, 0, 0, 0))
    faces = pl.BlockSpec((CHUNK, 8, 128), lambda i: (i, 0, 0))
    z_faces = pl.BlockSpec((CHUNK // 2, 8, 128), lambda i: (i, 0, 0))
    edges = pl.BlockSpec((1, 8, 128), lambda i: (i, 0, 0))
    fm_spec = pl.BlockSpec((CHUNK, 128), lambda i: (i, 0))
    shape = jax.ShapeDtypeStruct
    face_shape = shape((count, 8, 128), F32)
    z_shape = shape((count // 2, 8, 128), F32)
    edge_shape = shape((steps, 8, 128), F32)
    local, left, right, z, el, er, inv = pl.pallas_call(
        compute_kernel,
        grid=(steps,),
        in_specs=[
            blocks,
            pl.BlockSpec((CHUNK, EZ, 3, 2, 8, 128), lambda i: (i, 0, 0, 0, 0, 0)),
            vmem,
            vmem,
            fm_spec,
            smem,
        ],
        out_specs=[blocks, faces, faces, z_faces, edges, edges, smem],
        out_shape=[
            shape((count, EZ, 2, 8, 128), F32),
            face_shape,
            face_shape,
            z_shape,
            edge_shape,
            edge_shape,
            shape((2 * count,), jnp.int32),
        ],
    )(u, m, matrices, vectors, face_map, slab_ids)
    left_in, right_in, z_in, el_in, er_in = pl.pallas_call(
        exchange_kernel,
        in_specs=[vmem] * 5,
        out_specs=[vmem] * 5,
        out_shape=[face_shape, face_shape, z_shape, edge_shape, edge_shape],
        scratch_shapes=[pltpu.SemaphoreType.DMA((5,)), pltpu.SemaphoreType.DMA((5,))],
        compiler_params=pltpu.CompilerParams(collective_id=0, has_side_effects=True),
    )(left, right, z, el, er)
    out = pl.pallas_call(
        final_kernel,
        grid=(steps,),
        in_specs=[blocks, vmem, vmem, z_faces, vmem, vmem, fm_spec, smem, smem],
        out_specs=blocks,
        out_shape=shape((count, EZ, 2, 8, 128), F32),
    )(local, left_in, right_in, z_in, el_in, er_in, face_map, slab_ids, inv)
    out = out.reshape(count, EZ, 2, 2, EY, 128).transpose(0, 1, 4, 2, 3, 5)
    return out.reshape(1, count, EZ, EY, PTS)


def solution(mesh):
    return jax.shard_map(
        body,
        mesh=mesh,
        in_specs=(
            P("layer", "slab", None, None, None),
            P("layer", "slab", None, None, None, None),
            P(),
            P("slab", None),
        ),
        out_specs=P("layer", "slab", None, None, None),
        check_vma=False,
    )
```

profile of v0, /device:TPU:1, one launch (start us, length us, event | category | flops | bytes accessed | tf_op | source)
XLA Modules:
  0.0 56.8 jit_solution(15971335177103109495)
XLA Ops:
  0.0 31.3 %shard_map.64 = (f32[64,4,2,8,128]{4,3,2,1,0:T(8,128)}, f32[64,8,128]{2,1,0:T(8,128)}, f32[64,8,128]{2,1,0:T(8,128)}, f32[32,8,128]{2,1,0:T(8,128)}, f32[8,8,128...) custom-call(f32[64,4,2,8,128]{4,3,2,1,0:T(8,128)} %bitcast.16, f32[64,4,3,2,8,128]{5,4,3,2,1,0:T(8,128)} %bitcast.15, ...), custom_call_target="tpu_custom_call" | custom-call | tf_op jit(solution)/shard_map/pallas_call | solution.py:331
  31.3 18.0 %shard_map.65 = (f32[64,8,128]{2,1,0:T(8,128)}, f32[64,8,128]{2,1,0:T(8,128)}, f32[32,8,128]{2,1,0:T(8,128)}, f32[8,8,128]{2,1,0:T(8,128)}, f32[8,8,128]{2,1,0:T(8,128)}) custom-call(f32[64,8,128]{2,1,0:T(8,128)} %get-tuple-element.18.left, f32[64,8,128]{2,1,0:T(8,128)} %get-tuple-element.19.right, f32[32,8,128]{2,1,0:T(8,128)} %get-tuple-element.20.z, ...), custom_call_target="tpu_custom_call" | custom-call | tf_op jit(solution)/shard_map/pallas_call | solution.py:353
  49.3 7.5 %shard_map.66 = f32[64,4,2,8,128]{4,3,2,1,0:T(8,128)} custom-call(f32[64,4,2,8,128]{4,3,2,1,0:T(8,128)} %get-tuple-element.17.local_ref, f32[64,8,128]{2,1,0:T(8,128)} %get-tuple-element.23.left_in, f32[64,8,128]{2,1,0:T(8,128)} %get-tuple-element.24.right_in, f32[32,8,128]{2,1,0:T(8,128)} %get-tuple-element.25.z_in, f32[8,8,128]{2,1,0:T(8,128)} %get-tuple-element.26.el_in, ...), custom_call_target="tpu_custom_call" | custom-call | tf_op jit(solution)/shard_map/pallas_call | solution.py:361
where the time goes:
time: 57.1 us; the launch traced here: 56.8 us
  Pallas kernels  56.8 us (99%)
    pallas_call x1, Pallas kernels, body(): pl.pallas_call(compute_kernel, grid=(steps,), in_specs=[blocks, pl.BlockS...  31.3 us
    pallas_call x1, Pallas kernels, body(): pl.pallas_call(exchange_kernel, in_specs=[vmem] * 5, out_specs=[vmem] * 5...  18 us
    pallas_call x1, Pallas kernels, body(): pl.pallas_call(final_kernel, grid=(steps,), in_specs=[blocks, vmem, vmem,...  7.51 us

commit v1 on v0

v1 whole, which is shorter than its diff:
```python
import functools

import jax
import jax.numpy as jnp
import numpy as np
from jax import lax
from jax.experimental import pallas as pl
from jax.experimental.pallas import tpu as pltpu
from jax.sharding import PartitionSpec as P

P_SIZE = 8
PTS = 512
EY = 4
EZ = 4
CHUNK = 8
F32 = jnp.float32
BF16 = jnp.bfloat16
MESH = pl.DeviceIdType.MESH


def legendre_pair(gll_nodes, degree):
    lower_poly = gll_nodes * 0.0 + 1.0
    upper_poly = gll_nodes.copy()
    for poly_order in range(2, degree + 1):
        lower_poly, upper_poly = (
            upper_poly,
            ((2 * poly_order - 1) * gll_nodes * upper_poly - (poly_order - 1) * lower_poly)
            / poly_order,
        )
    return (lower_poly, upper_poly)


def gll_tables():
    degree = P_SIZE - 1
    gll_nodes = -np.cos(np.pi * np.arange(P_SIZE) / degree)
    for newton_sweep in range(100):
        lower_poly, upper_poly = legendre_pair(gll_nodes, degree)
        gll_nodes = gll_nodes - (gll_nodes * upper_poly - lower_poly) / ((degree + 1) * upper_poly)
    lower_poly, upper_poly = legendre_pair(gll_nodes, degree)
    quad_weights = 2.0 / (degree * (degree + 1) * upper_poly * upper_poly)
    identity = np.eye(P_SIZE)
    differ = gll_nodes[:, None] - gll_nodes[None, :] + identity
    derivative = upper_poly[:, None] / (upper_poly[None, :] * differ)
    derivative = derivative * (1.0 - identity)
    derivative[0, 0] = -degree * (degree + 1) / 4.0
    derivative[degree, degree] = degree * (degree + 1) / 4.0
    return derivative, quad_weights


def parts(table):
    high = np.asarray(table, np.float32).astype(BF16)
    low = (table - high.astype(np.float64)).astype(np.float32).astype(BF16)
    return high, low


def constant_tables():
    derivative, rho = gll_tables()
    eye = np.eye(P_SIZE)
    pair = np.eye(2)
    x_in = np.kron(pair, np.kron(eye, derivative.T))
    y_in = np.kron(pair, np.kron(derivative.T, eye))
    x_out = np.kron(pair, np.kron(eye, derivative))
    y_out = np.kron(pair, np.kron(derivative, eye))
    high, low = parts(np.concatenate([x_in, y_in], 1))
    matrices = [high, low]
    for table in (x_out, y_out):
        matrices.append(np.concatenate(parts(table), 1))
    sub = np.arange(8)[:, None] // 4
    lane = np.arange(128)[None, :]
    c_low = 2 * sub + lane // 64
    vectors = []
    for table in (derivative, derivative.T):
        for half in range(2):
            for source in range(2):
                for move in (0, 2, 1, 3):
                    vectors.append(table[4 * half + c_low, 4 * source + (c_low ^ move)])
    plane = rho[lane // 8 % 8] * rho[lane % 8]
    for half in range(2):
        vectors.append(rho[4 * half + c_low] * plane)
    return np.stack(matrices), np.stack(vectors).astype(np.float32)


def turn(value, shift):
    return pltpu.roll(value, shift % 128, axis=value.ndim - 1) if shift % 128 else value


def slide(value, shift):
    return pltpu.roll(value, shift % 8, axis=value.ndim - 2)


def mirror(value):
    return slide(turn(value, 64), 4)


def iotas():
    sub = lax.broadcasted_iota(jnp.int32, (8, 128), 0)
    lane = lax.broadcasted_iota(jnp.int32, (8, 128), 1)
    return sub, lane


def split(value):
    high = value.astype(BF16)
    low = (value - high.astype(F32)).astype(BF16)
    return jnp.concatenate([high, low], axis=-1)


def product(both, matrix):
    return jnp.dot(both, jnp.concatenate([matrix, matrix], 0), preferred_element_type=F32)


def along_z(low, high, low_turned, high_turned, table_ref, start):
    terms = []
    for value, turned in ((low, low_turned), (high, high_turned)):
        terms += [value, slide(value, 4), turned, slide(turned, 4)]
    out = []
    for half in range(2):
        total = table_ref[start + 8 * half] * terms[0]
        for k in range(1, 8):
            total += table_ref[start + 8 * half + k] * terms[k]
        out.append(total)
    return out


def flip_faces(value, sub, lane):
    value = jnp.take_along_axis(value, sub ^ 3, axis=0)
    return jnp.take_along_axis(value, lane ^ 56, axis=1)


def edge_mask(sub, lane, slot):
    base = jnp.where(sub < 4, 0, 71)
    return ((lane - base - slot) & 71) == 0


def chunk_local(u_ref, m_ref, mat_ref, vec_ref, flip_mask, sub, lane):
    count = u_ref.shape[0]
    rows = count * EZ * 2 * 8
    u = u_ref[...].reshape(rows, 128)
    both = split(u)
    grads = product(both, mat_ref[0]) + product(both, mat_ref[1])
    weights = [vec_ref[32], vec_ref[33]]
    turned = turn(u, 64)
    flux_x, flux_y, flux_z = [], [], []
    for s in range(count):
        for ez in range(EZ):
            at = (s * EZ + ez) * 16
            pieces = along_z(
                u[at : at + 8], u[at + 8 : at + 16], turned[at : at + 8], turned[at + 8 : at + 16], vec_ref, 0
            )
            for h in range(2):
                grad = grads[at + 8 * h : at + 8 * h + 8]
                flux_z.append(pieces[h] * (weights[h] * m_ref[s, ez, 2, h]))
                flux_x.append(grad[:, :128] * (weights[h] * m_ref[s, ez, 0, h]))
                flux_y.append(grad[:, 128:] * (weights[h] * m_ref[s, ez, 1, h]))
    flux_turned = [turn(value, 64) for value in flux_z]
    out_z = [
        along_z(flux_z[k], flux_z[k + 1], flux_turned[k], flux_turned[k + 1], vec_ref, 16)
        for k in range(0, 2 * count * EZ, 2)
    ]
    result = product(split(jnp.concatenate(flux_x, 0)), mat_ref[2])
    result += product(split(jnp.concatenate(flux_y, 0)), mat_ref[3])

    b = (lane >> 3) & 7
    a = lane & 7
    ey = sub & 3
    high_b = (b == 7) & (ey < 3)
    low_b = (b == 0) & (ey > 0)
    bottom = (sub < 4) & (lane < 64)
    top = (sub >= 4) & (lane >= 64)
    diagonal = bottom | top
    local, lefts, rights, z_own = [], [], [], []
    for s in range(count):
        block = []
        for ez in range(EZ):
            for h in range(2):
                at = (s * EZ + ez) * 16 + 8 * h
                v = result[at : at + 8, :128] + result[at : at + 8, 128:] + out_z[s * EZ + ez][h]
                after = turn(slide(v, -1), 56)
                before = turn(slide(v, 1), -56)
                block.append(v + jnp.where(high_b, after, jnp.where(low_b, before, 0.0)))
        for ez in range(EZ - 1):
            upper, lower = block[2 * ez + 1], block[2 * ez + 2]
            block[2 * ez + 2] = jnp.where(bottom, lower + mirror(upper), lower)
            block[2 * ez + 1] = jnp.where(top, upper + mirror(lower), upper)
        left, right = block[0], turn(block[7], 0)
        for j in range(1, 8):
            left = jnp.where(a == j, turn(block[j], j), left)
        for j in range(7):
            right = jnp.where(a == j, turn(block[j], j - 7), right)
        right = jnp.where(flip_mask(s), flip_faces(right, sub, lane), right)
        local.append(block)
        lefts.append(left)
        rights.append(right)
        z_own.append(jnp.where(bottom, block[0], block[7]))
    z_pairs = [
        jnp.where(diagonal, z_own[s], turn(z_own[s + 1], 64)) for s in range(0, count, 2)
    ]
    edges = []
    for faces in (lefts, rights):
        packed = faces[0]
        for s in range(1, count):
            packed = jnp.where(edge_mask(sub, lane, s), turn(faces[s], s), packed)
        moved = slide(packed, 4)
        edges.append(jnp.where(sub < 4, turn(moved, -71), turn(moved, 71)))
    return local, lefts, rights, z_pairs, edges


def chunk_final(local_ref, left_in, right_in, z_in, put):
    sub, lane = iotas()
    a = lane & 7
    bottom = (sub < 4) & (lane < 64)
    top = (sub >= 4) & (lane >= 64)
    count = local_ref.shape[0]
    for s in range(count):
        left, right, z = left_in(s), right_in(s), z_in(s)
        for j in range(8):
            v = local_ref[s, j // 2, j % 2]
            v += jnp.where(a == 0, turn(left, -j), jnp.where(a == 7, turn(right, 7 - j), 0.0))
            if j == 0:
                v += jnp.where(bottom, z, 0.0)
            if j == 7:
                v += jnp.where(top, z, 0.0)
            put(s, j, v)


def positions(wanted, values, offset, count):
    t = lax.broadcasted_iota(jnp.int32, (count, 128), 0)
    lane = lax.broadcasted_iota(jnp.int32, (count, 128), 1)
    column = jnp.sum(jnp.where(lane == t + offset, values, 0).astype(F32), axis=1, keepdims=True)
    hit = column == wanted.astype(F32)
    return jnp.sum(jnp.where(hit, t, 0).astype(F32), axis=0, keepdims=True).astype(jnp.int32)


def main_kernel(
    u_hbm, m_hbm, mat_hbm, vec_hbm, fm_hbm, ids_hbm,
    local, left_in, right_in, z_in, el_in, er_in, fm, pos,
    u_v, m_v, mat, vec, ids, pos_v, left, right, z, el, er,
    in_sem, one_sem, send_sem, recv_sem,
):
    cycle = lax.axis_size("slab")
    me = lax.axis_index("slab")
    layer = lax.axis_index("layer")
    after, before = lax.rem(me + 1, cycle), lax.rem(me + cycle - 1, cycle)
    other = 1 - layer
    peers = [(after, layer), (before, layer), (me, other), (after, other), (before, other)]
    count = local.shape[0]
    steps = count // CHUNK
    total = cycle * count
    barrier = pltpu.get_barrier_semaphore()
    for s, l in peers:
        pl.semaphore_signal(barrier, inc=1, device_id={"slab": s, "layer": l}, device_id_type=MESH)

    def loads(i):
        part = pl.ds(i * CHUNK, CHUNK)
        return [
            pltpu.make_async_copy(u_hbm.at[part], u_v.at[part], in_sem.at[0, i]),
            pltpu.make_async_copy(m_hbm.at[part], m_v.at[part], in_sem.at[1, i]),
        ]

    def once():
        pairs = [(mat_hbm, mat), (vec_hbm, vec), (fm_hbm.at[:, pl.ds(0, 128)], fm), (ids_hbm, ids)]
        return [pltpu.make_async_copy(a, b, one_sem.at[k]) for k, (a, b) in enumerate(pairs)]

    for copy in loads(0) + once():
        copy.start()
    for i in range(1, steps):
        for copy in loads(i):
            copy.start()
    for copy in once():
        copy.wait()

    per_row = 128 // count
    rows = [ids[pl.ds(d // per_row, 1), :] for d in (me, before, after)]
    sub, lane = iotas()
    found = []
    for row, device, move in ((rows[1], before, total - 1), (rows[2], after, 1)):
        wanted = rows[0] + move
        wanted = jnp.where(wanted >= total, wanted - total, wanted)
        found.append(positions(wanted, row, lax.rem(device, per_row) * count, count))
    pos_v[...] = jnp.where(sub == 0, found[0], found[1])
    pos_copy = pltpu.make_async_copy(pos_v, pos, one_sem.at[4])
    pos_copy.start()

    def sends(i, chunks):
        part = pl.ds(i * CHUNK, chunks * CHUNK)
        half = pl.ds(i * (CHUNK // 2), chunks * (CHUNK // 2))
        single = pl.ds(i, chunks)
        jobs = [(right, right_in, part), (left, left_in, part), (z, z_in, half), (er, er_in, single), (el, el_in, single)]
        return [
            pltpu.make_async_remote_copy(
                src_ref=src.at[at],
                dst_ref=dst.at[at],
                send_sem=send_sem.at[k],
                recv_sem=recv_sem.at[k],
                device_id={"slab": s, "layer": l},
                device_id_type=MESH,
            )
            for k, ((src, dst, at), (s, l)) in enumerate(zip(jobs, peers))
        ]

    pl.semaphore_wait(barrier, 5)

    def step(i, carry):
        for copy in loads(i):
            copy.wait()

        def flip_mask(s):
            return fm[pl.ds(i * CHUNK + s, 1), :] != lane

        blocks, lefts, rights, z_pairs, edges = chunk_local(
            u_v.at[pl.ds(i * CHUNK, CHUNK)], m_v.at[pl.ds(i * CHUNK, CHUNK)], mat, vec, flip_mask, sub, lane
        )
        for s in range(CHUNK):
            for j in range(8):
                local[i * CHUNK + s, j // 2, j % 2] = blocks[s][j]
            left[i * CHUNK + s] = lefts[s]
            right[i * CHUNK + s] = rights[s]
        for s in range(CHUNK // 2):
            z[i * (CHUNK // 2) + s] = z_pairs[s]
        el[i] = edges[0]
        er[i] = edges[1]
        for copy in sends(i, 1):
            copy.start()
        return carry

    lax.fori_loop(0, steps, step, 0)

    pos_copy.wait()
    for copy in sends(0, steps):
        copy.wait()


def final_kernel(local, left_in, right_in, z_in, el_in, er_in, fm, pos, out_hbm, out, sem):
    sub, lane = iotas()
    count = local.shape[0]
    steps = count // CHUNK
    per_row = 128 // count
    first = lax.rem(lax.axis_index("slab"), per_row) * count
    on_edge = edge_mask(sub, lane, 0)

    def write(i):
        part = pl.ds(i * CHUNK, CHUNK)
        return pltpu.make_async_copy(out.at[part], out_hbm.at[part], sem.at[i])

    def fetch(face_ref, edge_ref, at):
        packed = pltpu.roll(edge_ref[at >> 3], (128 - (at & 7)) & 127, axis=1)
        return face_ref[at] + jnp.where(on_edge, packed, 0.0)

    def step(i, carry):
        base = i * CHUNK

        def get_left(s):
            return fetch(right_in, er_in, pos[0, first + base + s])

        def get_right(s):
            value = fetch(left_in, el_in, pos[1, first + base + s])
            return jnp.where(fm[pl.ds(base + s, 1), :] != lane, flip_faces(value, sub, lane), value)

        def get_z(s):
            value = slide(z_in[i * (CHUNK // 2) + s // 2], 4)
            return value if s % 2 else turn(value, 64)

        def put(s, j, value):
            out[base + s, j // 2, j % 2] = value

        chunk_final(local.at[pl.ds(base, CHUNK)], get_left, get_right, get_z, put)
        write(i).start()
        return carry

    lax.fori_loop(0, steps, step, 0)

    def finish(i, carry):
        write(i).wait()
        return carry

    lax.fori_loop(0, steps, finish, 0)


def body(nodal_field, metric, slab_ids, face_map):
    count = nodal_field.shape[1]
    steps = count // CHUNK
    u = nodal_field.reshape(count, EZ, EY, 2, 2, 128).transpose(0, 1, 3, 4, 2, 5)
    u = u.reshape(count, EZ, 2, 8, 128)
    m = metric.reshape(count, EZ, EY, 3, 2, 2, 128).transpose(0, 1, 3, 4, 5, 2, 6)
    m = m.reshape(count, EZ, 3, 2, 8, 128)
    ids = slab_ids.reshape(-1, 128)
    matrices, vectors = constant_tables()
    matrices, vectors = jnp.asarray(matrices), jnp.asarray(vectors)
    hbm = pl.BlockSpec(memory_space=pltpu.HBM)
    vmem = pl.BlockSpec(memory_space=pltpu.VMEM)
    smem = pl.BlockSpec(memory_space=pltpu.SMEM)
    whole = (count, EZ, 2, 8, 128)
    face, z_face, edge = (count, 8, 128), (count // 2, 8, 128), (steps, 8, 128)
    dma = pltpu.SemaphoreType.DMA
    shared = pl.pallas_call(
        main_kernel,
        in_specs=[hbm] * 6,
        out_specs=[vmem] * 7 + [smem],
        out_shape=[pltpu.VMEM(s, F32) for s in (whole, face, face, z_face, edge, edge)]
        + [pltpu.VMEM((count, 128), jnp.int32), pltpu.SMEM((8, 128), jnp.int32)],
        scratch_shapes=[
            pltpu.VMEM(u.shape, F32),
            pltpu.VMEM(m.shape, F32),
            pltpu.VMEM(matrices.shape, BF16),
            pltpu.VMEM(vectors.shape, F32),
            pltpu.VMEM(ids.shape, jnp.int32),
            pltpu.VMEM((8, 128), jnp.int32),
            pltpu.VMEM(face, F32),
            pltpu.VMEM(face, F32),
            pltpu.VMEM(z_face, F32),
            pltpu.VMEM(edge, F32),
            pltpu.VMEM(edge, F32),
            dma((2, steps)),
            dma((5,)),
            dma((5,)),
            dma((5,)),
        ],
        compiler_params=pltpu.CompilerParams(
            collective_id=0, has_side_effects=True, vmem_limit_bytes=60 * 2**20
        ),
    )(u, m, matrices, vectors, face_map, ids)
    out = pl.pallas_call(
        final_kernel,
        in_specs=[vmem] * 7 + [smem],
        out_specs=hbm,
        out_shape=jax.ShapeDtypeStruct(whole, F32),
        scratch_shapes=[pltpu.VMEM(whole, F32), dma((steps,))],
        compiler_params=pltpu.CompilerParams(vmem_limit_bytes=40 * 2**20),
    )(*shared)
    out = out.reshape(count, EZ, 2, 2, EY, 128).transpose(0, 1, 4, 2, 3, 5)
    return out.reshape(1, count, EZ, EY, PTS)


def solution(mesh):
    return jax.shard_map(
        body,
        mesh=mesh,
        in_specs=(
            P("layer", "slab", None, None, None),
            P("layer", "slab", None, None, None, None),
            P(),
            P("slab", None),
        ),
        out_specs=P("layer", "slab", None, None, None),
        check_vma=False,
    )
```

time: 57.1 us -> 28 us (0.49)
  Pallas kernels: 56.8 us -> 27.9 us
    pallas_call x3 -> x2, Pallas kernels: 56.8 us -> 27.9 us  [the longest x1 24.4 us: body(): pl.pallas_call(main_kernel, in_specs=[hbm] * 6, out_specs=[vmem] * 7 + [s...]
where the time goes in v1:
time: 28 us; the launch traced here: 27.9 us
  Pallas kernels  27.9 us (100%)
    pallas_call x1, Pallas kernels, body(): pl.pallas_call(main_kernel, in_specs=[hbm] * 6, out_specs=[vmem] * 7 + [s...  24.4 us
    pallas_call x1, Pallas kernels, body(): pl.pallas_call(final_kernel, in_specs=[vmem] * 7 + [smem], out_specs=hbm,...  3.5 us

profile of v1, /device:TPU:1, one launch (start us, length us, event | category | flops | bytes accessed | tf_op | source)
XLA Modules:
  0.0 27.9 jit_solution(8633279542769247623)
XLA Ops:
  0.0 24.4 %shard_map.64 = (f32[64,4,2,8,128]{4,3,2,1,0:T(8,128)S(1)}, f32[64,8,128]{2,1,0:T(8,128)S(1)}, f32[64,8,128]{2,1,0:T(8,128)S(1)}, f32[32,8,128]{2,1,0:T(8,128)S(...) custom-call(f32[64,4,2,8,128]{4,3,2,1,0:T(8,128)} %bitcast.17, ...), custom_call_target="tpu_custom_call" | custom-call | tf_op jit(solution)/shard_map/pallas_call | solution.py:394
  24.4 3.5 %shard_map.65 = f32[64,4,2,8,128]{4,3,2,1,0:T(8,128)} custom-call(f32[64,4,2,8,128]{4,3,2,1,0:T(8,128)S(1)} %get-tuple-element.13.local, f32[64,8,128]{2,1,0:T(8,128)S(1)} %get-tuple-element.14.left_in, f32[64,8,128]{2,1,0:T(8,128)S(1)} %get-tuple-element.15.right_in, f32[32,8,128]{2,1,0:T(8,128)S(1)} %get-tuple-element.16.z_in, ...), custom_call_target="tpu_custom_call" | custom-call | tf_op jit(solution)/shard_map/pallas_call | solution.py:421

commit v2 on v1

--- a/solution.py
+++ b/solution.py
@@ -13,6 +13,8 @@
 EY = 4
 EZ = 4
 CHUNK = 8
+LAST = 16
+GATHER = 16
 F32 = jnp.float32
 BF16 = jnp.bfloat16
 MESH = pl.DeviceIdType.MESH
@@ -121,9 +123,9 @@
     return out
 
 
-def flip_faces(value, sub, lane):
+def flip_faces(value, sub, lane, shift):
     value = jnp.take_along_axis(value, sub ^ 3, axis=0)
-    return jnp.take_along_axis(value, lane ^ 56, axis=1)
+    return jnp.take_along_axis(value, ((((lane - shift) & 127) ^ 56) + shift) & 127, axis=1)
 
 
 def edge_mask(sub, lane, slot):
@@ -131,7 +133,7 @@
     return ((lane - base - slot) & 71) == 0
 
 
-def chunk_local(u_ref, m_ref, mat_ref, vec_ref, flip_mask, sub, lane):
+def chunk_fluxes(u_ref, m_ref, mat_ref, vec_ref, fx_ref, fy_ref, fz_ref):
     count = u_ref.shape[0]
     rows = count * EZ * 2 * 8
     u = u_ref[...].reshape(rows, 128)
@@ -139,7 +141,7 @@
     grads = product(both, mat_ref[0]) + product(both, mat_ref[1])
     weights = [vec_ref[32], vec_ref[33]]
     turned = turn(u, 64)
-    flux_x, flux_y, flux_z = [], [], []
+    flux_x, flux_y = [], []
     for s in range(count):
         for ez in range(EZ):
             at = (s * EZ + ez) * 16
@@ -148,20 +150,26 @@
             )
             for h in range(2):
                 grad = grads[at + 8 * h : at + 8 * h + 8]
-                flux_z.append(pieces[h] * (weights[h] * m_ref[s, ez, 2, h]))
+                fz_ref[at // 8 + h] = pieces[h] * (weights[h] * m_ref[s, ez, 2, h])
                 flux_x.append(grad[:, :128] * (weights[h] * m_ref[s, ez, 0, h]))
                 flux_y.append(grad[:, 128:] * (weights[h] * m_ref[s, ez, 1, h]))
+    fx_ref[...] = split(jnp.concatenate(flux_x, 0))
+    fy_ref[...] = split(jnp.concatenate(flux_y, 0))
+
+
+def chunk_local(fx_ref, fy_ref, fz_ref, mat_ref, vec_ref, flip_mask, sub, lane):
+    count = CHUNK
+    result = product(fx_ref[...], mat_ref[2]) + product(fy_ref[...], mat_ref[3])
+    flux_z = [fz_ref[k] for k in range(2 * count * EZ)]
     flux_turned = [turn(value, 64) for value in flux_z]
     out_z = [
         along_z(flux_z[k], flux_z[k + 1], flux_turned[k], flux_turned[k + 1], vec_ref, 16)
         for k in range(0, 2 * count * EZ, 2)
     ]
-    result = product(split(jnp.concatenate(flux_x, 0)), mat_ref[2])
-    result += product(split(jnp.concatenate(flux_y, 0)), mat_ref[3])
-
     b = (lane >> 3) & 7
     a = lane & 7
     ey = sub & 3
+    swap = jnp.where((b == 0) | (b == 7), lane ^ 56, lane)
     high_b = (b == 7) & (ey < 3)
     low_b = (b == 0) & (ey > 0)
     bottom = (sub < 4) & (lane < 64)
@@ -174,19 +182,19 @@
             for h in range(2):
                 at = (s * EZ + ez) * 16 + 8 * h
                 v = result[at : at + 8, :128] + result[at : at + 8, 128:] + out_z[s * EZ + ez][h]
-                after = turn(slide(v, -1), 56)
-                before = turn(slide(v, 1), -56)
-                block.append(v + jnp.where(high_b, after, jnp.where(low_b, before, 0.0)))
+                swapped = jnp.take_along_axis(v, swap, axis=1)
+                met = jnp.where(high_b, slide(swapped, -1), jnp.where(low_b, slide(swapped, 1), 0.0))
+                block.append(v + met)
         for ez in range(EZ - 1):
             upper, lower = block[2 * ez + 1], block[2 * ez + 2]
             block[2 * ez + 2] = jnp.where(bottom, lower + mirror(upper), lower)
             block[2 * ez + 1] = jnp.where(top, upper + mirror(lower), upper)
-        left, right = block[0], turn(block[7], 0)
+        left = right = block[0]
         for j in range(1, 8):
-            left = jnp.where(a == j, turn(block[j], j), left)
-        for j in range(7):
-            right = jnp.where(a == j, turn(block[j], j - 7), right)
-        right = jnp.where(flip_mask(s), flip_faces(right, sub, lane), right)
+            moved = turn(block[j], j)
+            left = jnp.where(a == j, moved, left)
+            right = jnp.where(a == j - 1, moved, right)
+        right = jnp.where(flip_mask(s), flip_faces(right, sub, lane, 7), right)
         local.append(block)
         lefts.append(left)
         rights.append(right)
@@ -195,31 +203,13 @@
         jnp.where(diagonal, z_own[s], turn(z_own[s + 1], 64)) for s in range(0, count, 2)
     ]
     edges = []
-    for faces in (lefts, rights):
+    for faces, shift in ((lefts, 0), (rights, 7)):
         packed = faces[0]
         for s in range(1, count):
-            packed = jnp.where(edge_mask(sub, lane, s), turn(faces[s], s), packed)
+            packed = jnp.where(edge_mask(sub, lane, s + shift), turn(faces[s], s), packed)
         moved = slide(packed, 4)
-        edges.append(jnp.where(sub < 4, turn(moved, -71), turn(moved, 71)))
+        edges.append(jnp.where(sub < 4, turn(moved, -71 - shift), turn(moved, 71 - shift)))
     return local, lefts, rights, z_pairs, edges
-
-
-def chunk_final(local_ref, left_in, right_in, z_in, put):
-    sub, lane = iotas()
-    a = lane & 7
-    bottom = (sub < 4) & (lane < 64)
-    top = (sub >= 4) & (lane >= 64)
-    count = local_ref.shape[0]
-    for s in range(count):
-        left, right, z = left_in(s), right_in(s), z_in(s)
-        for j in range(8):
-            v = local_ref[s, j // 2, j % 2]
-            v += jnp.where(a == 0, turn(left, -j), jnp.where(a == 7, turn(right, 7 - j), 0.0))
-            if j == 0:
-                v += jnp.where(bottom, z, 0.0)
-            if j == 7:
-                v += jnp.where(top, z, 0.0)
-            put(s, j, v)
 
 
 def positions(wanted, values, offset, count):
@@ -233,7 +223,7 @@
 def main_kernel(
     u_hbm, m_hbm, mat_hbm, vec_hbm, fm_hbm, ids_hbm,
     local, left_in, right_in, z_in, el_in, er_in, fm, pos,
-    u_v, m_v, mat, vec, ids, pos_v, left, right, z, el, er,
+    u_v, m_v, fx, fy, fz, mat, vec, ids, pos_v, left, right, z, el, er,
     in_sem, one_sem, send_sem, recv_sem,
 ):
     cycle = lax.axis_size("slab")
@@ -297,18 +287,17 @@
             for k, ((src, dst, at), (s, l)) in enumerate(zip(jobs, peers))
         ]
 
-    pl.semaphore_wait(barrier, 5)
-
-    def step(i, carry):
+    def fluxes(i):
         for copy in loads(i):
             copy.wait()
-
+        part = pl.ds(i * CHUNK, CHUNK)
+        chunk_fluxes(u_v.at[part], m_v.at[part], mat, vec, fx, fy, fz)
+
+    def assemble(i):
         def flip_mask(s):
             return fm[pl.ds(i * CHUNK + s, 1), :] != lane
 
-        blocks, lefts, rights, z_pairs, edges = chunk_local(
-            u_v.at[pl.ds(i * CHUNK, CHUNK)], m_v.at[pl.ds(i * CHUNK, CHUNK)], mat, vec, flip_mask, sub, lane
-        )
+        blocks, lefts, rights, z_pairs, edges = chunk_local(fx, fy, fz, mat, vec, flip_mask, sub, lane)
         for s in range(CHUNK):
             for j in range(8):
                 local[i * CHUNK + s, j // 2, j % 2] = blocks[s][j]
@@ -318,61 +307,86 @@
             z[i * (CHUNK // 2) + s] = z_pairs[s]
         el[i] = edges[0]
         er[i] = edges[1]
+
+    def launch(i):
         for copy in sends(i, 1):
             copy.start()
+
+    fluxes(0)
+    pl.semaphore_wait(barrier, 5)
+
+    def step(i, carry):
+        for copy in loads(i):
+            copy.wait()
+        assemble(i - 1)
+        part = pl.ds(i * CHUNK, CHUNK)
+        chunk_fluxes(u_v.at[part], m_v.at[part], mat, vec, fx, fy, fz)
+        launch(i - 1)
         return carry
 
-    lax.fori_loop(0, steps, step, 0)
-
+    lax.fori_loop(1, steps, step, 0)
+    assemble(steps - 1)
+    launch(steps - 1)
     pos_copy.wait()
     for copy in sends(0, steps):
         copy.wait()
 
 
-def final_kernel(local, left_in, right_in, z_in, el_in, er_in, fm, pos, out_hbm, out, sem):
+def final_kernel(local, left_in, right_in, z_in, el_in, er_in, fm, pos, out_hbm, out, faces, sem):
     sub, lane = iotas()
     count = local.shape[0]
-    steps = count // CHUNK
     per_row = 128 // count
     first = lax.rem(lax.axis_index("slab"), per_row) * count
     on_edge = edge_mask(sub, lane, 0)
+    even = (lane & 1) == 0
+    a = lane & 7
+    on_face = (a == 0) | (a == 7)
+    bottom = (sub < 4) & (lane < 64)
+    top = (sub >= 4) & (lane >= 64)
 
     def write(i):
-        part = pl.ds(i * CHUNK, CHUNK)
+        part = pl.ds(i * LAST, LAST)
         return pltpu.make_async_copy(out.at[part], out_hbm.at[part], sem.at[i])
 
-    def fetch(face_ref, edge_ref, at):
-        packed = pltpu.roll(edge_ref[at >> 3], (128 - (at & 7)) & 127, axis=1)
-        return face_ref[at] + jnp.where(on_edge, packed, 0.0)
+    def edge(edge_ref, at):
+        return jnp.where(on_edge, pltpu.roll(edge_ref[at >> 3], (128 - (at & 7)) & 127, axis=1), 0.0)
+
+    def gather(i, carry):
+        for s in range(GATHER):
+            slab = i * GATHER + s
+            back, ahead = pos[0, first + slab], pos[1, first + slab]
+            low = turn(right_in[back], -7) + edge(er_in, back)
+            high = left_in[ahead] + edge(el_in, ahead)
+            flipped = fm[pl.ds(slab, 1), :] != lane
+            high = turn(jnp.where(flipped, flip_faces(high, sub, lane, 0), high), 7)
+            faces[slab, 0] = jnp.where(even, low, high)
+            faces[slab, 1] = jnp.where(even, high, low)
+        return carry
+
+    lax.fori_loop(0, count // GATHER, gather, 0)
 
     def step(i, carry):
-        base = i * CHUNK
-
-        def get_left(s):
-            return fetch(right_in, er_in, pos[0, first + base + s])
-
-        def get_right(s):
-            value = fetch(left_in, el_in, pos[1, first + base + s])
-            return jnp.where(fm[pl.ds(base + s, 1), :] != lane, flip_faces(value, sub, lane), value)
-
-        def get_z(s):
-            value = slide(z_in[i * (CHUNK // 2) + s // 2], 4)
-            return value if s % 2 else turn(value, 64)
-
-        def put(s, j, value):
-            out[base + s, j // 2, j % 2] = value
-
-        chunk_final(local.at[pl.ds(base, CHUNK)], get_left, get_right, get_z, put)
+        for s in range(LAST):
+            slab = i * LAST + s
+            z = slide(z_in[i * (LAST // 2) + s // 2], 4)
+            z = z if s % 2 else turn(z, 64)
+            for j in range(8):
+                v = local[slab, j // 2, j % 2] + jnp.where(on_face, turn(faces[slab, j % 2], -j), 0.0)
+                if j == 0:
+                    v += jnp.where(bottom, z, 0.0)
+                if j == 7:
+                    v += jnp.where(top, z, 0.0)
+                out[slab, j // 2, j % 2] = v
         write(i).start()
         return carry
 
-    lax.fori_loop(0, steps, step, 0)
+    lax.fori_loop(0, count // LAST, step, 0)
 
     def finish(i, carry):
         write(i).wait()
         return carry
 
-    lax.fori_loop(0, steps, finish, 0)
+    lax.fori_loop(0, count // LAST, finish, 0)
 
 
 def body(nodal_field, metric, slab_ids, face_map):
@@ -400,6 +414,9 @@
         scratch_shapes=[
             pltpu.VMEM(u.shape, F32),
             pltpu.VMEM(m.shape, F32),
+            pltpu.VMEM((CHUNK * EZ * 16, 256), BF16),
+            pltpu.VMEM((CHUNK * EZ * 16, 256), BF16),
+            pltpu.VMEM((CHUNK * EZ * 2, 8, 128), F32),
             pltpu.VMEM(matrices.shape, BF16),
             pltpu.VMEM(vectors.shape, F32),
             pltpu.VMEM(ids.shape, jnp.int32),
@@ -423,7 +440,7 @@
         in_specs=[vmem] * 7 + [smem],
         out_specs=hbm,
         out_shape=jax.ShapeDtypeStruct(whole, F32),
-        scratch_shapes=[pltpu.VMEM(whole, F32), dma((steps,))],
+        scratch_shapes=[pltpu.VMEM(whole, F32), pltpu.VMEM((count, 2, 8, 128), F32), dma((count // LAST,))],
         compiler_params=pltpu.CompilerParams(vmem_limit_bytes=40 * 2**20),
     )(*shared)
     out = out.reshape(count, EZ, 2, 2, EY, 128).transpose(0, 1, 4, 2, 3, 5)

time: 28 us -> 24.4 us (0.87)
  Pallas kernels: 27.9 us -> 24.3 us
    pallas_call x1, Pallas kernels: 24.4 us -> 21.6 us  [body(): pl.pallas_call(main_kernel, in_specs=[hbm] * 6, out_specs=[vmem] * 7 + [s...]
    pallas_call x1, Pallas kernels: 3.5 us -> 2.69 us  [body(): pl.pallas_call(final_kernel, in_specs=[vmem] * 7 + [smem], out_specs=hbm,...]
where the time goes in v2:
time: 24.4 us; the launch traced here: 24.3 us
  Pallas kernels  24.3 us (100%)
    pallas_call x1, Pallas kernels, body(): pl.pallas_call(main_kernel, in_specs=[hbm] * 6, out_specs=[vmem] * 7 + [s...  21.6 us
    pallas_call x1, Pallas kernels, body(): pl.pallas_call(final_kernel, in_specs=[vmem] * 7 + [smem], out_specs=hbm,...  2.69 us

profile of v2, /device:TPU:1, one launch (start us, length us, event | category | flops | bytes accessed | tf_op | source)
XLA Modules:
  0.0 24.3 jit_solution(10819267827185749620)
XLA Ops:
  0.0 21.6 %shard_map.64 = (f32[64,4,2,8,128]{4,3,2,1,0:T(8,128)S(1)}, f32[64,8,128]{2,1,0:T(8,128)S(1)}, f32[64,8,128]{2,1,0:T(8,128)S(1)}, f32[32,8,128]{2,1,0:T(8,128)S(...) custom-call(f32[64,4,2,8,128]{4,3,2,1,0:T(8,128)} %bitcast.17, ...), custom_call_target="tpu_custom_call" | custom-call | tf_op jit(solution)/shard_map/pallas_call | solution.py:408
  21.6 2.7 %shard_map.65 = f32[64,4,2,8,128]{4,3,2,1,0:T(8,128)} custom-call(f32[64,4,2,8,128]{4,3,2,1,0:T(8,128)S(1)} %get-tuple-element.13.local, f32[64,8,128]{2,1,0:T(8,128)S(1)} %get-tuple-element.14.left_in, f32[64,8,128]{2,1,0:T(8,128)S(1)} %get-tuple-element.15.right_in, f32[32,8,128]{2,1,0:T(8,128)S(1)} %get-tuple-element.16.z_in, ...), custom_call_target="tpu_custom_call" | custom-call | tf_op jit(solution)/shard_map/pallas_call | solution.py:438

commit v3 on v2

--- a/solution.py
+++ b/solution.py
@@ -13,8 +13,11 @@
 EY = 4
 EZ = 4
 CHUNK = 8
+AHEAD = 3
+HOLD = 3
+FACES, EDGES, BOTH = (0, 1, 2), (3, 4), (0, 1, 2, 3, 4)
 LAST = 16
-GATHER = 16
+GATHER = 32
 F32 = jnp.float32
 BF16 = jnp.bfloat16
 MESH = pl.DeviceIdType.MESH
@@ -86,6 +89,10 @@
     return pltpu.roll(value, shift % 128, axis=value.ndim - 1) if shift % 128 else value
 
 
+def spin(value, shift):
+    return pltpu.roll(value, (shift + 256) & 127, axis=1)
+
+
 def slide(value, shift):
     return pltpu.roll(value, shift % 8, axis=value.ndim - 2)
 
@@ -157,7 +164,7 @@
     fy_ref[...] = split(jnp.concatenate(flux_y, 0))
 
 
-def chunk_local(fx_ref, fy_ref, fz_ref, mat_ref, vec_ref, flip_mask, sub, lane):
+def chunk_local(fx_ref, fy_ref, fz_ref, mat_ref, vec_ref, flip_mask, sub, lane, offset):
     count = CHUNK
     result = product(fx_ref[...], mat_ref[2]) + product(fy_ref[...], mat_ref[3])
     flux_z = [fz_ref[k] for k in range(2 * count * EZ)]
@@ -208,7 +215,7 @@
         for s in range(1, count):
             packed = jnp.where(edge_mask(sub, lane, s + shift), turn(faces[s], s), packed)
         moved = slide(packed, 4)
-        edges.append(jnp.where(sub < 4, turn(moved, -71 - shift), turn(moved, 71 - shift)))
+        edges.append(jnp.where(sub < 4, spin(moved, offset - 71 - shift), spin(moved, offset + 71 - shift)))
     return local, lefts, rights, z_pairs, edges
 
 
@@ -252,7 +259,7 @@
 
     for copy in loads(0) + once():
         copy.start()
-    for i in range(1, steps):
+    for i in range(1, AHEAD):
         for copy in loads(i):
             copy.start()
     for copy in once():
@@ -270,10 +277,10 @@
     pos_copy = pltpu.make_async_copy(pos_v, pos, one_sem.at[4])
     pos_copy.start()
 
-    def sends(i, chunks):
+    def sends(i, chunks, kinds):
         part = pl.ds(i * CHUNK, chunks * CHUNK)
         half = pl.ds(i * (CHUNK // 2), chunks * (CHUNK // 2))
-        single = pl.ds(i, chunks)
+        single = pl.ds(i // 2, chunks // 2)
         jobs = [(right, right_in, part), (left, left_in, part), (z, z_in, half), (er, er_in, single), (el, el_in, single)]
         return [
             pltpu.make_async_remote_copy(
@@ -285,6 +292,7 @@
                 device_id_type=MESH,
             )
             for k, ((src, dst, at), (s, l)) in enumerate(zip(jobs, peers))
+            if k in kinds
         ]
 
     def fluxes(i):
@@ -297,7 +305,9 @@
         def flip_mask(s):
             return fm[pl.ds(i * CHUNK + s, 1), :] != lane
 
-        blocks, lefts, rights, z_pairs, edges = chunk_local(fx, fy, fz, mat, vec, flip_mask, sub, lane)
+        blocks, lefts, rights, z_pairs, edges = chunk_local(
+            fx, fy, fz, mat, vec, flip_mask, sub, lane, lax.rem(i, 2) * 64
+        )
         for s in range(CHUNK):
             for j in range(8):
                 local[i * CHUNK + s, j // 2, j % 2] = blocks[s][j]
@@ -305,19 +315,40 @@
             right[i * CHUNK + s] = rights[s]
         for s in range(CHUNK // 2):
             z[i * (CHUNK // 2) + s] = z_pairs[s]
-        el[i] = edges[0]
-        er[i] = edges[1]
+        first_of_two = jnp.where(sub < 4, lane, (lane - 71) & 127) < 64
+        odd = lax.rem(i, 2) == 1
+        for ref, edge in ((el, edges[0]), (er, edges[1])):
+            held = ref[i // 2]
+            ref[i // 2] = jnp.where(odd, jnp.where(first_of_two, held, edge), edge)
 
     def launch(i):
-        for copy in sends(i, 1):
-            copy.start()
+        @pl.when(i == HOLD)
+        def _():
+            pl.semaphore_wait(barrier, 5)
+            for copy in sends(0, HOLD + 1, BOTH):
+                copy.start()
+
+        @pl.when((i > HOLD) & (lax.rem(i, 2) == 0))
+        def _():
+            for copy in sends(i, 1, FACES):
+                copy.start()
+
+        @pl.when((i > HOLD) & (lax.rem(i, 2) == 1))
+        def _():
+            for copy in sends(i, 1, FACES) + sends(i - 1, 2, EDGES):
+                copy.start()
 
     fluxes(0)
-    pl.semaphore_wait(barrier, 5)
 
     def step(i, carry):
         for copy in loads(i):
             copy.wait()
+
+        @pl.when(i + AHEAD - 1 < steps)
+        def _():
+            for copy in loads(i + AHEAD - 1):
+                copy.start()
+
         assemble(i - 1)
         part = pl.ds(i * CHUNK, CHUNK)
         chunk_fluxes(u_v.at[part], m_v.at[part], mat, vec, fx, fy, fz)
@@ -326,9 +357,10 @@
 
     lax.fori_loop(1, steps, step, 0)
     assemble(steps - 1)
-    launch(steps - 1)
+    for copy in sends(steps - 1, 1, FACES) + sends(steps - 2, 2, EDGES):
+        copy.start()
     pos_copy.wait()
-    for copy in sends(0, steps):
+    for copy in sends(0, steps, BOTH):
         copy.wait()
 
 
@@ -349,7 +381,8 @@
         return pltpu.make_async_copy(out.at[part], out_hbm.at[part], sem.at[i])
 
     def edge(edge_ref, at):
-        return jnp.where(on_edge, pltpu.roll(edge_ref[at >> 3], (128 - (at & 7)) & 127, axis=1), 0.0)
+        slot = ((at & 8) << 3) | (at & 7)
+        return jnp.where(on_edge, pltpu.roll(edge_ref[at >> 4], (128 - slot) & 127, axis=1), 0.0)
 
     def gather(i, carry):
         for s in range(GATHER):
@@ -403,7 +436,7 @@
     vmem = pl.BlockSpec(memory_space=pltpu.VMEM)
     smem = pl.BlockSpec(memory_space=pltpu.SMEM)
     whole = (count, EZ, 2, 8, 128)
-    face, z_face, edge = (count, 8, 128), (count // 2, 8, 128), (steps, 8, 128)
+    face, z_face, edge = (count, 8, 128), (count // 2, 8, 128), (steps // 2, 8, 128)
     dma = pltpu.SemaphoreType.DMA
     shared = pl.pallas_call(
         main_kernel,

time: 24.4 us -> 22.4 us (0.918)
  the two profiles are of different devices: /device:TPU:1 before, /device:TPU:0 now
where the time goes in v3:
time: 22.4 us; the launch traced here: 22.3 us
  Pallas kernels  22.3 us (100%)
    pallas_call x1, Pallas kernels, body(): pl.pallas_call(main_kernel, in_specs=[hbm] * 6, out_specs=[vmem] * 7 + [s...  19.8 us
    pallas_call x1, Pallas kernels, body(): pl.pallas_call(final_kernel, in_specs=[vmem] * 7 + [smem], out_specs=hbm,...  2.47 us

profile of v3, /device:TPU:0, one launch (start us, length us, event | category | flops | bytes accessed | tf_op | source)
XLA Modules:
  0.0 22.3 jit_solution(12258756546231139846)
XLA Ops:
  0.0 19.8 %shard_map.64 = (f32[64,4,2,8,128]{4,3,2,1,0:T(8,128)S(1)}, f32[64,8,128]{2,1,0:T(8,128)S(1)}, f32[64,8,128]{2,1,0:T(8,128)S(1)}, f32[32,8,128]{2,1,0:T(8,128)S(...) custom-call(f32[64,4,2,8,128]{4,3,2,1,0:T(8,128)} %bitcast.17, ...), custom_call_target="tpu_custom_call" | custom-call | tf_op jit(solution)/shard_map/pallas_call | solution.py:441
  19.8 2.5 %shard_map.65 = f32[64,4,2,8,128]{4,3,2,1,0:T(8,128)} custom-call(f32[64,4,2,8,128]{4,3,2,1,0:T(8,128)S(1)} %get-tuple-element.13.local, f32[64,8,128]{2,1,0:T(8,128)S(1)} %get-tuple-element.14.left_in, f32[64,8,128]{2,1,0:T(8,128)S(1)} %get-tuple-element.15.right_in, f32[32,8,128]{2,1,0:T(8,128)S(1)} %get-tuple-element.16.z_in, ...), custom_call_target="tpu_custom_call" | custom-call | tf_op jit(solution)/shard_map/pallas_call | solution.py:471

commit v4 on v3

--- a/solution.py
+++ b/solution.py
@@ -66,22 +66,23 @@
     y_in = np.kron(pair, np.kron(derivative.T, eye))
     x_out = np.kron(pair, np.kron(eye, derivative))
     y_out = np.kron(pair, np.kron(derivative, eye))
-    high, low = parts(np.concatenate([x_in, y_in], 1))
+    lane = np.arange(128)[None, :]
+    plane = rho[lane // 8 % 8] * rho[lane % 8]
+    high, low = parts(np.concatenate([x_in * plane, y_in * plane], 1))
     matrices = [high, low]
     for table in (x_out, y_out):
         matrices.append(np.concatenate(parts(table), 1))
     sub = np.arange(8)[:, None] // 4
-    lane = np.arange(128)[None, :]
     c_low = 2 * sub + lane // 64
     vectors = []
-    for table in (derivative, derivative.T):
-        for half in range(2):
-            for source in range(2):
-                for move in (0, 2, 1, 3):
-                    vectors.append(table[4 * half + c_low, 4 * source + (c_low ^ move)])
-    plane = rho[lane // 8 % 8] * rho[lane % 8]
+    for table, weight in ((derivative, rho[c_low] * plane), (derivative.T, 1.0)):
+        for sign in (1.0, -1.0):
+            for move in (0, 1, 2, 3):
+                other = c_low ^ move
+                term = weight * (table[c_low, other] + sign * table[c_low, 7 - other]) / 2
+                vectors.append(np.roll(term, 4, 0) if move > 1 else term)
     for half in range(2):
-        vectors.append(rho[4 * half + c_low] * plane)
+        vectors.append(rho[4 * half + c_low] + 0.0 * plane)
     return np.stack(matrices), np.stack(vectors).astype(np.float32)
 
 
@@ -118,16 +119,17 @@
 
 
 def along_z(low, high, low_turned, high_turned, table_ref, start):
-    terms = []
-    for value, turned in ((low, low_turned), (high, high_turned)):
-        terms += [value, slide(value, 4), turned, slide(turned, 4)]
-    out = []
-    for half in range(2):
-        total = table_ref[start + 8 * half] * terms[0]
-        for k in range(1, 8):
-            total += table_ref[start + 8 * half + k] * terms[k]
-        out.append(total)
-    return out
+    back, back_turned = slide(high_turned, 4), slide(high, 4)
+    halves = []
+    for value, turned, first in (
+        (low + back, low_turned + back_turned, start),
+        (low - back, low_turned - back_turned, start + 4),
+    ):
+        near = table_ref[first] * value + table_ref[first + 1] * turned
+        far = table_ref[first + 2] * value + table_ref[first + 3] * turned
+        halves.append(near + slide(far, 4))
+    even, odd = halves
+    return even + odd, mirror(odd - even)
 
 
 def flip_faces(value, sub, lane, shift):
@@ -144,9 +146,9 @@
     count = u_ref.shape[0]
     rows = count * EZ * 2 * 8
     u = u_ref[...].reshape(rows, 128)
-    both = split(u)
+    scaled = u.reshape(count * EZ, 2, 8, 128) * vec_ref[16:18]
+    both = split(scaled.reshape(rows, 128))
     grads = product(both, mat_ref[0]) + product(both, mat_ref[1])
-    weights = [vec_ref[32], vec_ref[33]]
     turned = turn(u, 64)
     flux_x, flux_y = [], []
     for s in range(count):
@@ -157,32 +159,32 @@
             )
             for h in range(2):
                 grad = grads[at + 8 * h : at + 8 * h + 8]
-                fz_ref[at // 8 + h] = pieces[h] * (weights[h] * m_ref[s, ez, 2, h])
-                flux_x.append(grad[:, :128] * (weights[h] * m_ref[s, ez, 0, h]))
-                flux_y.append(grad[:, 128:] * (weights[h] * m_ref[s, ez, 1, h]))
+                fz_ref[at // 8 + h] = pieces[h] * m_ref[s, ez, 2, h]
+                flux_x.append(grad[:, :128] * m_ref[s, ez, 0, h])
+                flux_y.append(grad[:, 128:] * m_ref[s, ez, 1, h])
     fx_ref[...] = split(jnp.concatenate(flux_x, 0))
     fy_ref[...] = split(jnp.concatenate(flux_y, 0))
 
 
-def chunk_local(fx_ref, fy_ref, fz_ref, mat_ref, vec_ref, flip_mask, sub, lane, offset):
+def corners(sub, lane):
+    return (sub < 4) & (lane < 64), (sub >= 4) & (lane >= 64)
+
+
+def chunk_local(fx_ref, fy_ref, fz_ref, mat_ref, vec_ref, sub, lane, put):
     count = CHUNK
     result = product(fx_ref[...], mat_ref[2]) + product(fy_ref[...], mat_ref[3])
     flux_z = [fz_ref[k] for k in range(2 * count * EZ)]
     flux_turned = [turn(value, 64) for value in flux_z]
     out_z = [
-        along_z(flux_z[k], flux_z[k + 1], flux_turned[k], flux_turned[k + 1], vec_ref, 16)
+        along_z(flux_z[k], flux_z[k + 1], flux_turned[k], flux_turned[k + 1], vec_ref, 8)
         for k in range(0, 2 * count * EZ, 2)
     ]
     b = (lane >> 3) & 7
-    a = lane & 7
     ey = sub & 3
     swap = jnp.where((b == 0) | (b == 7), lane ^ 56, lane)
     high_b = (b == 7) & (ey < 3)
     low_b = (b == 0) & (ey > 0)
-    bottom = (sub < 4) & (lane < 64)
-    top = (sub >= 4) & (lane >= 64)
-    diagonal = bottom | top
-    local, lefts, rights, z_own = [], [], [], []
+    bottom, top = corners(sub, lane)
     for s in range(count):
         block = []
         for ez in range(EZ):
@@ -196,18 +198,27 @@
             upper, lower = block[2 * ez + 1], block[2 * ez + 2]
             block[2 * ez + 2] = jnp.where(bottom, lower + mirror(upper), lower)
             block[2 * ez + 1] = jnp.where(top, upper + mirror(lower), upper)
-        left = right = block[0]
+        for j in range(8):
+            put(s, j, block[j])
+
+
+def chunk_pack(stage_ref, flip_mask, sub, lane, offset):
+    count = CHUNK
+    a = lane & 7
+    bottom, top = corners(sub, lane)
+    lefts, rights, z_own = [], [], []
+    for s in range(count):
+        left = right = stage_ref[s, 0]
         for j in range(1, 8):
-            moved = turn(block[j], j)
+            moved = turn(stage_ref[s, j], j)
             left = jnp.where(a == j, moved, left)
             right = jnp.where(a == j - 1, moved, right)
         right = jnp.where(flip_mask(s), flip_faces(right, sub, lane, 7), right)
-        local.append(block)
         lefts.append(left)
         rights.append(right)
-        z_own.append(jnp.where(bottom, block[0], block[7]))
+        z_own.append(jnp.where(bottom, stage_ref[s, 0], stage_ref[s, 7]))
     z_pairs = [
-        jnp.where(diagonal, z_own[s], turn(z_own[s + 1], 64)) for s in range(0, count, 2)
+        jnp.where(bottom | top, z_own[s], turn(z_own[s + 1], 64)) for s in range(0, count, 2)
     ]
     edges = []
     for faces, shift in ((lefts, 0), (rights, 7)):
@@ -216,7 +227,7 @@
             packed = jnp.where(edge_mask(sub, lane, s + shift), turn(faces[s], s), packed)
         moved = slide(packed, 4)
         edges.append(jnp.where(sub < 4, spin(moved, offset - 71 - shift), spin(moved, offset + 71 - shift)))
-    return local, lefts, rights, z_pairs, edges
+    return lefts, rights, z_pairs, edges
 
 
 def positions(wanted, values, offset, count):
@@ -230,7 +241,7 @@
 def main_kernel(
     u_hbm, m_hbm, mat_hbm, vec_hbm, fm_hbm, ids_hbm,
     local, left_in, right_in, z_in, el_in, er_in, fm, pos,
-    u_v, m_v, fx, fy, fz, mat, vec, ids, pos_v, left, right, z, el, er,
+    u_v, m_v, fx, fy, fz, stage, mat, vec, ids, pos_v, left, right, z, el, er,
     in_sem, one_sem, send_sem, recv_sem,
 ):
     cycle = lax.axis_size("slab")
@@ -259,7 +270,7 @@
 
     for copy in loads(0) + once():
         copy.start()
-    for i in range(1, AHEAD):
+    for i in range(1, AHEAD - 1):
         for copy in loads(i):
             copy.start()
     for copy in once():
@@ -296,21 +307,22 @@
         ]
 
     def fluxes(i):
-        for copy in loads(i):
-            copy.wait()
         part = pl.ds(i * CHUNK, CHUNK)
         chunk_fluxes(u_v.at[part], m_v.at[part], mat, vec, fx, fy, fz)
 
     def assemble(i):
+        def put(s, j, value):
+            local[i * CHUNK + s, j // 2, j % 2] = value
+            stage[s, j] = value
+
+        chunk_local(fx, fy, fz, mat, vec, sub, lane, put)
+
+    def pack(i):
         def flip_mask(s):
             return fm[pl.ds(i * CHUNK + s, 1), :] != lane
 
-        blocks, lefts, rights, z_pairs, edges = chunk_local(
-            fx, fy, fz, mat, vec, flip_mask, sub, lane, lax.rem(i, 2) * 64
-        )
+        lefts, rights, z_pairs, edges = chunk_pack(stage, flip_mask, sub, lane, lax.rem(i, 2) * 64)
         for s in range(CHUNK):
-            for j in range(8):
-                local[i * CHUNK + s, j // 2, j % 2] = blocks[s][j]
             left[i * CHUNK + s] = lefts[s]
             right[i * CHUNK + s] = rights[s]
         for s in range(CHUNK // 2):
@@ -321,6 +333,15 @@
             held = ref[i // 2]
             ref[i // 2] = jnp.where(odd, jnp.where(first_of_two, held, edge), edge)
 
+    def arrive(i):
+        for copy in loads(i):
+            copy.wait()
+
+        @pl.when(i + AHEAD - 1 < steps)
+        def _():
+            for copy in loads(i + AHEAD - 1):
+                copy.start()
+
     def launch(i):
         @pl.when(i == HOLD)
         def _():
@@ -338,25 +359,26 @@
             for copy in sends(i, 1, FACES) + sends(i - 1, 2, EDGES):
                 copy.start()
 
+    arrive(0)
     fluxes(0)
+    arrive(1)
+    assemble(0)
+    fluxes(1)
 
     def step(i, carry):
-        for copy in loads(i):
-            copy.wait()
-
-        @pl.when(i + AHEAD - 1 < steps)
-        def _():
-            for copy in loads(i + AHEAD - 1):
-                copy.start()
-
+        arrive(i)
+        pack(i - 2)
         assemble(i - 1)
-        part = pl.ds(i * CHUNK, CHUNK)
-        chunk_fluxes(u_v.at[part], m_v.at[part], mat, vec, fx, fy, fz)
-        launch(i - 1)
+        fluxes(i)
+        launch(i - 2)
         return carry
 
-    lax.fori_loop(1, steps, step, 0)
+    lax.fori_loop(2, steps, step, 0)
+    pack(steps - 2)
     assemble(steps - 1)
+    for copy in sends(steps - 2, 1, FACES):
+        copy.start()
+    pack(steps - 1)
     for copy in sends(steps - 1, 1, FACES) + sends(steps - 2, 2, EDGES):
         copy.start()
     pos_copy.wait()
@@ -450,6 +472,7 @@
             pltpu.VMEM((CHUNK * EZ * 16, 256), BF16),
             pltpu.VMEM((CHUNK * EZ * 16, 256), BF16),
             pltpu.VMEM((CHUNK * EZ * 2, 8, 128), F32),
+            pltpu.VMEM((CHUNK, 8, 8, 128), F32),
             pltpu.VMEM(matrices.shape, BF16),
             pltpu.VMEM(vectors.shape, F32),
             pltpu.VMEM(ids.shape, jnp.int32),

time: 22.4 us -> 21.5 us (0.960)
  Pallas kernels: 22.3 us -> 21.4 us
    pallas_call x1, Pallas kernels: 19.8 us -> 18.9 us  [body(): pl.pallas_call(main_kernel, in_specs=[hbm] * 6, out_specs=[vmem] * 7 + [s...]
where the time goes in v4:
time: 21.5 us; the launch traced here: 21.4 us
  Pallas kernels  21.4 us (100%)
    pallas_call x1, Pallas kernels, body(): pl.pallas_call(main_kernel, in_specs=[hbm] * 6, out_specs=[vmem] * 7 + [s...  18.9 us
    pallas_call x1, Pallas kernels, body(): pl.pallas_call(final_kernel, in_specs=[vmem] * 7 + [smem], out_specs=hbm,...  2.47 us

profile of v4, /device:TPU:0, one launch (start us, length us, event | category | flops | bytes accessed | tf_op | source)
XLA Modules:
  0.0 21.4 jit_solution(12588535999745431944)
XLA Ops:
  0.0 18.9 %shard_map.64 = (f32[64,4,2,8,128]{4,3,2,1,0:T(8,128)S(1)}, f32[64,8,128]{2,1,0:T(8,128)S(1)}, f32[64,8,128]{2,1,0:T(8,128)S(1)}, f32[32,8,128]{2,1,0:T(8,128)S(...) custom-call(f32[64,4,2,8,128]{4,3,2,1,0:T(8,128)} %bitcast.17, ...), custom_call_target="tpu_custom_call" | custom-call | tf_op jit(solution)/shard_map/pallas_call | solution.py:463
  18.9 2.5 %shard_map.65 = f32[64,4,2,8,128]{4,3,2,1,0:T(8,128)} custom-call(f32[64,4,2,8,128]{4,3,2,1,0:T(8,128)S(1)} %get-tuple-element.13.local, f32[64,8,128]{2,1,0:T(8,128)S(1)} %get-tuple-element.14.left_in, f32[64,8,128]{2,1,0:T(8,128)S(1)} %get-tuple-element.15.right_in, f32[32,8,128]{2,1,0:T(8,128)S(1)} %get-tuple-element.16.z_in, ...), custom_call_target="tpu_custom_call" | custom-call | tf_op jit(solution)/shard_map/pallas_call | solution.py:494

commit v5 on v4

--- a/solution.py
+++ b/solution.py
@@ -13,8 +13,8 @@
 EY = 4
 EZ = 4
 CHUNK = 8
-AHEAD = 3
-HOLD = 3
+AHEAD = 4
+HOLD = 0
 FACES, EDGES, BOTH = (0, 1, 2), (3, 4), (0, 1, 2, 3, 4)
 LAST = 16
 GATHER = 32
@@ -91,7 +91,7 @@
 
 
 def spin(value, shift):
-    return pltpu.roll(value, (shift + 256) & 127, axis=1)
+    return turn(value, shift)
 
 
 def slide(value, shift):
@@ -254,14 +254,11 @@
     steps = count // CHUNK
     total = cycle * count
     barrier = pltpu.get_barrier_semaphore()
-    for s, l in peers:
-        pl.semaphore_signal(barrier, inc=1, device_id={"slab": s, "layer": l}, device_id_type=MESH)
-
     def loads(i):
         part = pl.ds(i * CHUNK, CHUNK)
         return [
-            pltpu.make_async_copy(u_hbm.at[part], u_v.at[part], in_sem.at[0, i]),
-            pltpu.make_async_copy(m_hbm.at[part], m_v.at[part], in_sem.at[1, i]),
+            pltpu.make_async_copy(u_hbm.at[part], u_v.at[part], in_sem.at[0, lax.rem(i, AHEAD)]),
+            pltpu.make_async_copy(m_hbm.at[part], m_v.at[part], in_sem.at[1, lax.rem(i, AHEAD)]),
         ]
 
     def once():
@@ -273,6 +270,8 @@
     for i in range(1, AHEAD - 1):
         for copy in loads(i):
             copy.start()
+    for s, l in peers:
+        pl.semaphore_signal(barrier, inc=1, device_id={"slab": s, "layer": l}, device_id_type=MESH)
     for copy in once():
         copy.wait()
 
@@ -317,21 +316,19 @@
 
         chunk_local(fx, fy, fz, mat, vec, sub, lane, put)
 
-    def pack(i):
+    def pack(i, odd):
         def flip_mask(s):
             return fm[pl.ds(i * CHUNK + s, 1), :] != lane
 
-        lefts, rights, z_pairs, edges = chunk_pack(stage, flip_mask, sub, lane, lax.rem(i, 2) * 64)
+        lefts, rights, z_pairs, edges = chunk_pack(stage, flip_mask, sub, lane, 64 * odd)
         for s in range(CHUNK):
             left[i * CHUNK + s] = lefts[s]
             right[i * CHUNK + s] = rights[s]
         for s in range(CHUNK // 2):
             z[i * (CHUNK // 2) + s] = z_pairs[s]
         first_of_two = jnp.where(sub < 4, lane, (lane - 71) & 127) < 64
-        odd = lax.rem(i, 2) == 1
         for ref, edge in ((el, edges[0]), (er, edges[1])):
-            held = ref[i // 2]
-            ref[i // 2] = jnp.where(odd, jnp.where(first_of_two, held, edge), edge)
+            ref[i // 2] = jnp.where(first_of_two, ref[i // 2], edge) if odd else edge
 
     def arrive(i):
         for copy in loads(i):
@@ -342,21 +339,16 @@
             for copy in loads(i + AHEAD - 1):
                 copy.start()
 
-    def launch(i):
-        @pl.when(i == HOLD)
+    def launch(k):
+        @pl.when(k == HOLD)
         def _():
             pl.semaphore_wait(barrier, 5)
-            for copy in sends(0, HOLD + 1, BOTH):
+            for copy in sends(0, 2 * (HOLD + 1), BOTH):
                 copy.start()
 
-        @pl.when((i > HOLD) & (lax.rem(i, 2) == 0))
+        @pl.when(k > HOLD)
         def _():
-            for copy in sends(i, 1, FACES):
-                copy.start()
-
-        @pl.when((i > HOLD) & (lax.rem(i, 2) == 1))
-        def _():
-            for copy in sends(i, 1, FACES) + sends(i - 1, 2, EDGES):
+            for copy in sends(2 * k, 2, BOTH):
                 copy.start()
 
     arrive(0)
@@ -365,20 +357,23 @@
     assemble(0)
     fluxes(1)
 
-    def step(i, carry):
-        arrive(i)
-        pack(i - 2)
-        assemble(i - 1)
-        fluxes(i)
-        launch(i - 2)
+    def step(k, carry):
+        arrive(2 * k)
+        arrive(2 * k + 1)
+        for odd in (0, 1):
+            i = 2 * k + odd
+            pack(i - 2, odd)
+            assemble(i - 1)
+            fluxes(i)
+        launch(k - 1)
         return carry
 
-    lax.fori_loop(2, steps, step, 0)
-    pack(steps - 2)
+    lax.fori_loop(1, steps // 2, step, 0)
+    pack(steps - 2, 0)
     assemble(steps - 1)
     for copy in sends(steps - 2, 1, FACES):
         copy.start()
-    pack(steps - 1)
+    pack(steps - 1, 1)
     for copy in sends(steps - 1, 1, FACES) + sends(steps - 2, 2, EDGES):
         copy.start()
     pos_copy.wait()
@@ -482,7 +477,7 @@
             pltpu.VMEM(z_face, F32),
             pltpu.VMEM(edge, F32),
             pltpu.VMEM(edge, F32),
-            dma((2, steps)),
+            dma((2, AHEAD)),
             dma((5,)),
             dma((5,)),
             dma((5,)),

time: 21.5 us -> 20.9 us (0.972)
  the two profiles are of different devices: /device:TPU:0 before, /device:TPU:1 now
where the time goes in v5:
time: 20.9 us; the launch traced here: 20.7 us
  Pallas kernels  20.7 us (99%)
    pallas_call x1, Pallas kernels, body(): pl.pallas_call(main_kernel, in_specs=[hbm] * 6, out_specs=[vmem] * 7 + [s...  18.2 us
    pallas_call x1, Pallas kernels, body(): pl.pallas_call(final_kernel, in_specs=[vmem] * 7 + [smem], out_specs=hbm,...  2.47 us

profile of v5, /device:TPU:1, one launch (start us, length us, event | category | flops | bytes accessed | tf_op | source)
XLA Modules:
  0.0 20.7 jit_solution(6425430530958687307)
XLA Ops:
  0.0 18.2 %shard_map.64 = (f32[64,4,2,8,128]{4,3,2,1,0:T(8,128)S(1)}, f32[64,8,128]{2,1,0:T(8,128)S(1)}, f32[64,8,128]{2,1,0:T(8,128)S(1)}, f32[32,8,128]{2,1,0:T(8,128)S(...) custom-call(f32[64,4,2,8,128]{4,3,2,1,0:T(8,128)} %bitcast.17, ...), custom_call_target="tpu_custom_call" | custom-call | tf_op jit(solution)/shard_map/pallas_call | solution.py:458
  18.2 2.5 %shard_map.65 = f32[64,4,2,8,128]{4,3,2,1,0:T(8,128)} custom-call(f32[64,4,2,8,128]{4,3,2,1,0:T(8,128)S(1)} %get-tuple-element.13.local, f32[64,8,128]{2,1,0:T(8,128)S(1)} %get-tuple-element.14.left_in, f32[64,8,128]{2,1,0:T(8,128)S(1)} %get-tuple-element.15.right_in, f32[32,8,128]{2,1,0:T(8,128)S(1)} %get-tuple-element.16.z_in, ...), custom_call_target="tpu_custom_call" | custom-call | tf_op jit(solution)/shard_map/pallas_call | solution.py:489

commit v6 on v5

--- a/solution.py
+++ b/solution.py
@@ -184,6 +184,7 @@
     swap = jnp.where((b == 0) | (b == 7), lane ^ 56, lane)
     high_b = (b == 7) & (ey < 3)
     low_b = (b == 0) & (ey > 0)
+    source = jnp.where(high_b, sub + 1, jnp.where(low_b, sub - 1, sub))
     bottom, top = corners(sub, lane)
     for s in range(count):
         block = []
@@ -192,8 +193,8 @@
                 at = (s * EZ + ez) * 16 + 8 * h
                 v = result[at : at + 8, :128] + result[at : at + 8, 128:] + out_z[s * EZ + ez][h]
                 swapped = jnp.take_along_axis(v, swap, axis=1)
-                met = jnp.where(high_b, slide(swapped, -1), jnp.where(low_b, slide(swapped, 1), 0.0))
-                block.append(v + met)
+                met = jnp.take_along_axis(swapped, source, axis=0)
+                block.append(v + jnp.where(high_b | low_b, met, 0.0))
         for ez in range(EZ - 1):
             upper, lower = block[2 * ez + 1], block[2 * ez + 2]
             block[2 * ez + 2] = jnp.where(bottom, lower + mirror(upper), lower)
@@ -240,8 +241,8 @@
 
 def main_kernel(
     u_hbm, m_hbm, mat_hbm, vec_hbm, fm_hbm, ids_hbm,
-    local, left_in, right_in, z_in, el_in, er_in, fm, pos,
-    u_v, m_v, fx, fy, fz, stage, mat, vec, ids, pos_v, left, right, z, el, er,
+    local, right_in, er_in, pos,
+    left_in, z_in, el_in, fm, u_v, m_v, fx, fy, fz, stage, highs, mat, vec, ids, pos_v, left, right, z, el, er,
     in_sem, one_sem, send_sem, recv_sem,
 ):
     cycle = lax.axis_size("slab")
@@ -272,20 +273,11 @@
             copy.start()
     for s, l in peers:
         pl.semaphore_signal(barrier, inc=1, device_id={"slab": s, "layer": l}, device_id_type=MESH)
-    for copy in once():
+    for copy in once()[:2]:
         copy.wait()
 
+    sub, lane = iotas()
     per_row = 128 // count
-    rows = [ids[pl.ds(d // per_row, 1), :] for d in (me, before, after)]
-    sub, lane = iotas()
-    found = []
-    for row, device, move in ((rows[1], before, total - 1), (rows[2], after, 1)):
-        wanted = rows[0] + move
-        wanted = jnp.where(wanted >= total, wanted - total, wanted)
-        found.append(positions(wanted, row, lax.rem(device, per_row) * count, count))
-    pos_v[...] = jnp.where(sub == 0, found[0], found[1])
-    pos_copy = pltpu.make_async_copy(pos_v, pos, one_sem.at[4])
-    pos_copy.start()
 
     def sends(i, chunks, kinds):
         part = pl.ds(i * CHUNK, chunks * CHUNK)
@@ -354,6 +346,17 @@
     arrive(0)
     fluxes(0)
     arrive(1)
+    for copy in once()[2:]:
+        copy.wait()
+    rows = [ids[pl.ds(d // per_row, 1), :] for d in (me, before, after)]
+    found = []
+    for row, device, move in ((rows[1], before, total - 1), (rows[2], after, 1)):
+        wanted = rows[0] + move
+        wanted = jnp.where(wanted >= total, wanted - total, wanted)
+        found.append(positions(wanted, row, lax.rem(device, per_row) * count, count))
+    pos_v[...] = jnp.where(sub == 0, found[0], found[1])
+    pos_copy = pltpu.make_async_copy(pos_v, pos, one_sem.at[4])
+    pos_copy.start()
     assemble(0)
     fluxes(1)
 
@@ -377,55 +380,72 @@
     for copy in sends(steps - 1, 1, FACES) + sends(steps - 2, 2, EDGES):
         copy.start()
     pos_copy.wait()
-    for copy in sends(0, steps, BOTH):
-        copy.wait()
-
-
-def final_kernel(local, left_in, right_in, z_in, el_in, er_in, fm, pos, out_hbm, out, faces, sem):
+    from_next = sends(0, steps, (1, 2, 4))
+    from_back = sends(0, steps, (0, 3))
+    for copy in from_next:
+        copy.wait_recv()
+    first = lax.rem(me, per_row) * count
+    on_edge = edge_mask(sub, lane, 0)
+    bottom, top = corners(sub, lane)
+    on_high = (lane & 7) == 7
+
+    def gather(i, carry):
+        for s in range(GATHER):
+            slab = i * GATHER + s
+            ahead = jnp.clip(pos[1, first + slab], 0, count - 1)
+            high = left_in[ahead] + edge_of(el_in, ahead, 0, on_edge)
+            flipped = fm[pl.ds(slab, 1), :] != lane
+            highs[slab] = jnp.where(flipped, flip_faces(high, sub, lane, 0), high)
+        return carry
+
+    lax.fori_loop(0, count // GATHER, gather, 0)
+
+    def add_high(i, carry):
+        for s in range(LAST):
+            slab = i * LAST + s
+            whole = z_in[i * (LAST // 2) + s // 2]
+            across = slide(whole, 4)
+            across = across if s % 2 else turn(across, 64)
+            for j in range(8):
+                v = local[slab, j // 2, j % 2] + jnp.where(on_high, turn(highs[slab], 7 - j), 0.0)
+                if j == 0:
+                    v += jnp.where(bottom, across, 0.0)
+                if j == 7:
+                    v += jnp.where(top, across, 0.0)
+                local[slab, j // 2, j % 2] = v
+        return carry
+
+    lax.fori_loop(0, count // LAST, add_high, 0)
+    for copy in from_back:
+        copy.wait_recv()
+    for copy in from_next + from_back:
+        copy.wait_send()
+
+
+def edge_of(edge_ref, at, shift, mask):
+    slot = ((at & 8) << 3) | (at & 7)
+    return jnp.where(mask, pltpu.roll(edge_ref[at >> 4], (128 + shift - slot) & 127, axis=1), 0.0)
+
+
+def final_kernel(local, right_in, er_in, pos, out_hbm, out, sem):
     sub, lane = iotas()
     count = local.shape[0]
     per_row = 128 // count
     first = lax.rem(lax.axis_index("slab"), per_row) * count
-    on_edge = edge_mask(sub, lane, 0)
-    even = (lane & 1) == 0
-    a = lane & 7
-    on_face = (a == 0) | (a == 7)
-    bottom = (sub < 4) & (lane < 64)
-    top = (sub >= 4) & (lane >= 64)
+    on_edge = edge_mask(sub, lane, 7)
+    on_low = (lane & 7) == 0
 
     def write(i):
         part = pl.ds(i * LAST, LAST)
         return pltpu.make_async_copy(out.at[part], out_hbm.at[part], sem.at[i])
 
-    def edge(edge_ref, at):
-        slot = ((at & 8) << 3) | (at & 7)
-        return jnp.where(on_edge, pltpu.roll(edge_ref[at >> 4], (128 - slot) & 127, axis=1), 0.0)
-
-    def gather(i, carry):
-        for s in range(GATHER):
-            slab = i * GATHER + s
-            back, ahead = pos[0, first + slab], pos[1, first + slab]
-            low = turn(right_in[back], -7) + edge(er_in, back)
-            high = left_in[ahead] + edge(el_in, ahead)
-            flipped = fm[pl.ds(slab, 1), :] != lane
-            high = turn(jnp.where(flipped, flip_faces(high, sub, lane, 0), high), 7)
-            faces[slab, 0] = jnp.where(even, low, high)
-            faces[slab, 1] = jnp.where(even, high, low)
-        return carry
-
-    lax.fori_loop(0, count // GATHER, gather, 0)
-
     def step(i, carry):
         for s in range(LAST):
             slab = i * LAST + s
-            z = slide(z_in[i * (LAST // 2) + s // 2], 4)
-            z = z if s % 2 else turn(z, 64)
+            back = jnp.clip(pos[0, first + slab], 0, count - 1)
+            low = right_in[back] + edge_of(er_in, back, 7, on_edge)
             for j in range(8):
-                v = local[slab, j // 2, j % 2] + jnp.where(on_face, turn(faces[slab, j % 2], -j), 0.0)
-                if j == 0:
-                    v += jnp.where(bottom, z, 0.0)
-                if j == 7:
-                    v += jnp.where(top, z, 0.0)
+                v = local[slab, j // 2, j % 2] + jnp.where(on_low, turn(low, -7 - j), 0.0)
                 out[slab, j // 2, j % 2] = v
         write(i).start()
         return carry
@@ -458,16 +478,20 @@
     shared = pl.pallas_call(
         main_kernel,
         in_specs=[hbm] * 6,
-        out_specs=[vmem] * 7 + [smem],
-        out_shape=[pltpu.VMEM(s, F32) for s in (whole, face, face, z_face, edge, edge)]
-        + [pltpu.VMEM((count, 128), jnp.int32), pltpu.SMEM((8, 128), jnp.int32)],
+        out_specs=[vmem] * 3 + [smem],
+        out_shape=[pltpu.VMEM(s, F32) for s in (whole, face, edge)] + [pltpu.SMEM((8, 128), jnp.int32)],
         scratch_shapes=[
+            pltpu.VMEM(face, F32),
+            pltpu.VMEM(z_face, F32),
+            pltpu.VMEM(edge, F32),
+            pltpu.VMEM((count, 128), jnp.int32),
             pltpu.VMEM(u.shape, F32),
             pltpu.VMEM(m.shape, F32),
             pltpu.VMEM((CHUNK * EZ * 16, 256), BF16),
             pltpu.VMEM((CHUNK * EZ * 16, 256), BF16),
             pltpu.VMEM((CHUNK * EZ * 2, 8, 128), F32),
             pltpu.VMEM((CHUNK, 8, 8, 128), F32),
+            pltpu.VMEM(face, F32),
             pltpu.VMEM(matrices.shape, BF16),
             pltpu.VMEM(vectors.shape, F32),
             pltpu.VMEM(ids.shape, jnp.int32),
@@ -488,10 +512,10 @@
     )(u, m, matrices, vectors, face_map, ids)
     out = pl.pallas_call(
         final_kernel,
-        in_specs=[vmem] * 7 + [smem],
+        in_specs=[vmem] * 3 + [smem],
         out_specs=hbm,
         out_shape=jax.ShapeDtypeStruct(whole, F32),
-        scratch_shapes=[pltpu.VMEM(whole, F32), pltpu.VMEM((count, 2, 8, 128), F32), dma((count // LAST,))],
+        scratch_shapes=[pltpu.VMEM(whole, F32), dma((count // LAST,))],
         compiler_params=pltpu.CompilerParams(vmem_limit_bytes=40 * 2**20),
     )(*shared)
     out = out.reshape(count, EZ, 2, 2, EY, 128).transpose(0, 1, 4, 2, 3, 5)

time: 20.9 us -> 20.5 us (0.981)
  Pallas kernels: 20.7 us -> 20.3 us
    pallas_call x2, Pallas kernels: 20.7 us -> 20.3 us  [the longest x1 18.2 us: body(): pl.pallas_call(main_kernel, in_specs=[hbm] * 6, out_specs=[vmem] * 3 + [s...]
where the time goes in v6:
time: 20.5 us; the launch traced here: 20.4 us
  Pallas kernels  20.3 us (99%)
    pallas_call x1, Pallas kernels, body(): pl.pallas_call(main_kernel, in_specs=[hbm] * 6, out_specs=[vmem] * 3 + [s...  18.2 us
    pallas_call x1, Pallas kernels, body(): pl.pallas_call(final_kernel, in_specs=[vmem] * 3 + [smem], out_specs=hbm,...  2.14 us

profile of v6, /device:TPU:1, one launch (start us, length us, event | category | flops | bytes accessed | tf_op | source)
XLA Modules:
  0.0 20.4 jit_solution(3362871577122970675)
XLA Ops:
  0.0 18.2 %shard_map.64 = (f32[64,4,2,8,128]{4,3,2,1,0:T(8,128)S(1)}, f32[64,8,128]{2,1,0:T(8,128)S(1)}, f32[4,8,128]{2,1,0:T(8,128)S(1)}, s32[8,128]{1,0:T(8,128)S(4)}) custom-call(f32[64,4,2,8,128]{4,3,2,1,0:T(8,128)} %bitcast.17, f32[64,4,3,2,8,128]{5,4,3,2,1,0:T(8,128)} %bitcast.16, bf16[4,128,256]{2,1,0:T(8,128)(2,1)} %constant.4.clone.mat_hbm, ...), custom_call_target="tpu_custom_call" | custom-call | tf_op jit(solution)/shard_map/pallas_call | solution.py:478
  18.2 2.1 %shard_map.65 = f32[64,4,2,8,128]{4,3,2,1,0:T(8,128)} custom-call(f32[64,4,2,8,128]{4,3,2,1,0:T(8,128)S(1)} %get-tuple-element.9.local, f32[64,8,128]{2,1,0:T(8,128)S(1)} %get-tuple-element.10.right_in, f32[4,8,128]{2,1,0:T(8,128)S(1)} %get-tuple-element.11.er_in, s32[8,128]{1,0:T(8,128)S(4)} %get-tuple-element.12.pos), custom_call_target="tpu_custom_call" | custom-call | tf_op jit(solution)/shard_map/pallas_call | solution.py:513

commit v7 on v6

--- a/solution.py
+++ b/solution.py
@@ -377,7 +377,7 @@
     for copy in sends(steps - 2, 1, FACES):
         copy.start()
     pack(steps - 1, 1)
-    for copy in sends(steps - 1, 1, FACES) + sends(steps - 2, 2, EDGES):
+    for copy in sends(steps - 1, 1, (0,)) + sends(steps - 2, 2, (3,)) + sends(steps - 1, 1, (1, 2)) + sends(steps - 2, 2, (4,)):
         copy.start()
     pos_copy.wait()
     from_next = sends(0, steps, (1, 2, 4))

time: 20.5 us -> 20.3 us (level)
  no operation moved by 1% of the time
where the time goes in v7:
time: 20.3 us; the launch traced here: 20.2 us
  Pallas kernels  20.2 us (100%)
    pallas_call x1, Pallas kernels, body(): pl.pallas_call(main_kernel, in_specs=[hbm] * 6, out_specs=[vmem] * 3 + [s...  18 us
    pallas_call x1, Pallas kernels, body(): pl.pallas_call(final_kernel, in_specs=[vmem] * 3 + [smem], out_specs=hbm,...  2.14 us

profile of v7, /device:TPU:1, one launch (start us, length us, event | category | flops | bytes accessed | tf_op | source)
XLA Modules:
  0.0 20.2 jit_solution(2311737976404202534)
XLA Ops:
  0.0 18.0 %shard_map.64 = (f32[64,4,2,8,128]{4,3,2,1,0:T(8,128)S(1)}, f32[64,8,128]{2,1,0:T(8,128)S(1)}, f32[4,8,128]{2,1,0:T(8,128)S(1)}, s32[8,128]{1,0:T(8,128)S(4)}) custom-call(f32[64,4,2,8,128]{4,3,2,1,0:T(8,128)} %bitcast.17, f32[64,4,3,2,8,128]{5,4,3,2,1,0:T(8,128)} %bitcast.16, bf16[4,128,256]{2,1,0:T(8,128)(2,1)} %constant.4.clone.mat_hbm, ...), custom_call_target="tpu_custom_call" | custom-call | tf_op jit(solution)/shard_map/pallas_call | solution.py:478
  18.0 2.1 %shard_map.65 = f32[64,4,2,8,128]{4,3,2,1,0:T(8,128)} custom-call(f32[64,4,2,8,128]{4,3,2,1,0:T(8,128)S(1)} %get-tuple-element.9.local, f32[64,8,128]{2,1,0:T(8,128)S(1)} %get-tuple-element.10.right_in, f32[4,8,128]{2,1,0:T(8,128)S(1)} %get-tuple-element.11.er_in, s32[8,128]{1,0:T(8,128)S(4)} %get-tuple-element.12.pos), custom_call_target="tpu_custom_call" | custom-call | tf_op jit(solution)/shard_map/pallas_call | solution.py:513
